TPU v7x, 32 devices: a whole 2x2x4 slice. The times are simulated.
32 devices in a mesh: tok: 4 (over z), out: 4 (over x, core), grp: 2 (over y).
Axes of the slice: x: 2, y: 2, z: 4, core: 2. Of those that a mesh axis runs over, the one named last changes fastest.
Arguments:
- activations: bfloat16 [1024, 2, 2048], P(('tok', 'grp'), None, 'out'), may hold values from -16 to 16
- out_grads: bfloat16 [1024, 2, 2048], P(('tok', 'grp'), None, 'out'), may hold values from -16 to 16
- weight: bfloat16 [2, 2048, 4096], P(None, 'out'), may hold values from -0.09375 to 0.09375
Outputs:
- update: bfloat16 [4096, 2, 2048], P(('tok', 'grp'), None, 'out')
- input_grad: bfloat16 [1024, 2, 2048], P(('tok', 'grp'), None, 'out')
All inputs are finite; a program needn't handle non-finite values.
Results may differ from a plain program's by a relative error of at most 0.0092.
Values may be sent and summed in bfloat16 or wider, within the bound.
A program may use at most 64 MiB of HBM per device.

v0:
```python
import math

import jax
import jax.numpy as jnp
from jax import lax
from jax.sharding import PartitionSpec as P

POWER = 3


DAMPING = 0.1
HIGH = lax.Precision.HIGHEST


def spread(piece):
    return lax.all_gather(piece, "out", axis=2, tiled=True)


def token_sums(maker, rows):
    return lax.psum_scatter(
        maker(jnp.int32(0), rows * lax.axis_size(("tok", "grp"))),
        ("tok", "grp"),
        scatter_dimension=0,
        tiled=True,
    )


def shared_rows(piece):
    return lax.all_gather(piece, ("tok", "grp"), axis=0, tiled=True)


def shared_total(vector):
    return lax.psum(vector, ("tok", "out", "grp"))


def diagonal_mask(rows, width, row_start, col_start):
    row_ids = row_start + lax.broadcasted_iota(jnp.int32, (rows, 1, width), 0)
    col_ids = col_start + lax.broadcasted_iota(jnp.int32, (rows, 1, width), 2)
    return jnp.where(row_ids == col_ids, 1.0, 0.0).astype(jnp.float32)


def multiply(left, right, gather_columns):
    row_band = spread(left)
    column_band = gather_columns(right)
    return jnp.einsum("rkj,jkc->rkc", row_band, column_band, preferred_element_type=jnp.float32)


def inverse_roots(tile, row_start, col_start, gather_columns, total):
    rows, count, width = tile.shape
    block = width * lax.axis_size("out")
    mask = diagonal_mask(rows, width, row_start, col_start)
    vector = jnp.ones((count, block), jnp.float32)
    image = vector
    for step in range(POWER):
        columns = lax.dynamic_slice_in_dim(vector, col_start, width, 1)
        part = jnp.einsum("rkc,kc->kr", tile, columns, precision=HIGH)
        placed = lax.dynamic_update_slice_in_dim(
            jnp.zeros((count, block), jnp.float32), part, row_start, 1
        )
        image = total(placed)
        if step + 1 < POWER:
            vector = image / jnp.sqrt(jnp.sum(image * image, axis=1, keepdims=True))
    scale = jnp.sum(vector * image, axis=1) / jnp.sum(vector * vector, axis=1)
    start = tile / scale[None, :, None]
    start_low = start.astype(jnp.bfloat16)
    first_low = ((3.0 * mask - start) / 2.0).astype(jnp.bfloat16)
    square_low = multiply(first_low, first_low, gather_columns).astype(jnp.bfloat16)
    moved = multiply(square_low, start_low, gather_columns)
    second_low = ((3.0 * mask - moved) / 2.0).astype(jnp.bfloat16)
    roots = multiply(first_low, second_low, gather_columns) / jnp.sqrt(scale)[None, :, None]
    return roots.astype(jnp.bfloat16)


def local(activations, out_grads, weight):
    tok_dev, blocks, width = activations.shape
    block = width * lax.axis_size("out")
    token_count = tok_dev * lax.axis_size("tok") * lax.axis_size("grp")
    col_start = lax.axis_index("out") * width
    local_sides = jnp.concatenate([activations, out_grads], axis=1)
    whole_sides = spread(local_sides)
    grads_whole = whole_sides[:, blocks:, :]
    weight_rows = weight.reshape(blocks, width, blocks, block)
    input_grad = jnp.einsum(
        "tjq,bcjq->tbc", grads_whole, weight_rows, preferred_element_type=jnp.float32
    ).astype(jnp.bfloat16)
    rows = block // (lax.axis_size("tok") * lax.axis_size("grp"))
    row_start = lax.axis_index(("tok", "grp")) * rows

    def shared_terms(start, span):
        return jnp.einsum(
            "tkr,tkc->rkc", whole_sides, local_sides, preferred_element_type=jnp.float32
        )

    sums = token_sums(shared_terms, rows)
    tile = sums / token_count + DAMPING * diagonal_mask(rows, width, row_start, col_start)
    roots = inverse_roots(tile, row_start, col_start, shared_rows, shared_total)
    bands = shared_rows(roots)
    whitened = jnp.einsum(
        "tkj,jkc->tkc", whole_sides, bands, preferred_element_type=jnp.float32
    ).astype(jnp.bfloat16)
    acts_whole = spread(whitened[:, :blocks, :]).reshape(tok_dev, blocks * block)
    grads_low = whitened[:, blocks:, :]
    owned_acts = lax.all_to_all(acts_whole, ("tok", "grp"), split_axis=1, concat_axis=0, tiled=True)
    update = jnp.einsum(
        "ta,tbc->abc",
        owned_acts,
        lax.all_gather(grads_low, ("tok", "grp"), axis=0, tiled=True),
        preferred_element_type=jnp.float32,
    )
    update = (update / math.sqrt(token_count)).astype(jnp.bfloat16)
    return (update, input_grad)


def solution(mesh):
    in_specs = (
        P(("tok", "grp"), None, "out"),
        P(("tok", "grp"), None, "out"),
        P(None, "out", None),
    )
    out_specs = (P(("tok", "grp"), None, "out"), P(("tok", "grp"), None, "out"))
    return jax.shard_map(local, mesh=mesh, in_specs=in_specs, out_specs=out_specs, check_vma=False)
```

profile of v0, /device:TPU:0, one launch (start us, length us, event | category | flops | bytes accessed | tf_op | source)
XLA Modules:
  0.0 1136.9 jit_solution(8817919165431428209)
XLA Ops:
  7.2 1.0 copy_dynamic-update-slice_fusion.1
  8.2 1.0 copy_dynamic-update-slice_fusion
  9.2 0.8 copy-done.1
  10.0 0.0 reduce-scatter.2.cloned.1.call-start
  10.0 25.4 %all-gather.10.cloned.1.call-done = bf16[128,4,2048]{2,0,1:T(8,128)(2,1)} async-done(((bf16[128,4,512]{2,0,1:T(8,128)(2,1)}), bf16[128,4,2048]{2,0,1:T(8,128)(2,1)}) %all-gather.10.cloned.1.call-update) | async-done | bytes 2097168 | tf_op jit(solution)/shard_map/all_gather | solution.py:16
  35.4 9.9 convolution_bitcast_fusion
  45.3 0.0 all-gather.16.cloned.1.call-start
  45.4 0.1 select_multiply_fusion.1
  45.6 280.1 %reduce-scatter.2.cloned.1.call-done = f32[256,4,512]{0,2,1:T(8,128)} async-done(((f32[2048,4,512]{0,2,1:T(8,128)}), f32[256,4,512]{0,2,1:T(8,128)}) %reduce-scatter.2.cloned.1.call-update) | async-done | bytes 2097168 | tf_op jit(solution)/shard_map/reduce_scatter | solution.py:20
  325.7 3.0 fusion.10
  328.7 39.4 %psum.21 = f32[4,2048]{1,0:T(4,128)S(1)} all-reduce(f32[4,2048]{1,0:T(4,128)S(1)} %bitcast_dynamic-update-slice_fusion.2), channel_id=1, replica_groups=mesh['tok'=4,'out'=4,'grp'=2] {'tok','out','grp'}, use_global_device_ids=true, to_apply=%region_1.2 | all-reduce | flops 8192 | bytes 65536 | tf_op jit(solution)/shard_map/psum | solution.py:33
  368.2 0.1 multiply_reduce_fusion.3
  368.3 0.1 fusion.26
  368.4 1.3 fusion.9
  369.8 39.9 %psum.22 = f32[4,2048]{1,0:T(4,128)S(1)} all-reduce(f32[4,2048]{1,0:T(4,128)S(1)} %bitcast_dynamic-update-slice_fusion.1), channel_id=1, replica_groups=mesh['tok'=4,'out'=4,'grp'=2] {'tok','out','grp'}, use_global_device_ids=true, to_apply=%region_3.4 | all-reduce | flops 8192 | bytes 65536 | tf_op jit(solution)/shard_map/psum | solution.py:33
  409.7 0.1 multiply_reduce_fusion.2
  409.9 0.1 broadcast_divide_fusion
  409.9 1.3 fusion.8
  411.3 40.3 %psum.23 = f32[4,2048]{1,0:T(4,128)S(1)} all-reduce(f32[4,2048]{1,0:T(4,128)S(1)} %bitcast_dynamic-update-slice_fusion), channel_id=1, replica_groups=mesh['tok'=4,'out'=4,'grp'=2] {'tok','out','grp'}, use_global_device_ids=true, to_apply=%region_5.6 | all-reduce | flops 8192 | bytes 65536 | tf_op jit(solution)/shard_map/psum | solution.py:33
  451.6 0.2 multiply_reduce_fusion
  451.8 1.8 multiply_convert_fusion.1
  453.7 0.5 all-gather.14.cloned.1.call-update
  454.2 0.5 all-gather.12.cloned.1.call-update
  454.8 33.2 %all-gather.16.cloned.1.call-done = bf16[256,4,2048]{0,2,1:T(8,128)(2,1)} async-done(((bf16[256,4,512]{0,2,1:T(8,128)(2,1)}), bf16[256,4,2048]{0,2,1:T(8,128)(2,1)}) %all-gather.16.cloned.1.call-update) | async-done | bytes 4194320 | tf_op jit(solution)/shard_map/all_gather | solution.py:16
  488.0 127.4 %all-gather.14.cloned.1.call-done = bf16[2048,4,512]{0,2,1:T(8,128)(2,1)} async-done(((bf16[256,4,512]{0,2,1:T(8,128)(2,1)}), bf16[2048,4,512]{0,2,1:T(8,128)(2,1)}) %all-gather.14.cloned.1.call-update) | async-done | bytes 8388624 | tf_op jit(solution)/shard_map/all_gather | solution.py:29
  615.5 7.9 fusion.5
  623.4 0.2 all-gather.20.cloned.1.call-start
  623.6 116.9 %all-gather.12.cloned.1.call-done = bf16[2048,4,512]{0,2,1:T(8,128)(2,1)} async-done(((bf16[256,4,512]{0,2,1:T(8,128)(2,1)}), bf16[2048,4,512]{0,2,1:T(8,128)(2,1)}) %all-gather.12.cloned.1.call-update) | async-done | bytes 8388624 | tf_op jit(solution)/shard_map/all_gather | solution.py:29
  740.5 34.7 %all-gather.18.cloned.1.call-done = bf16[256,4,2048]{0,2,1:T(8,128)(2,1)} async-done(((bf16[256,4,512]{0,2,1:T(8,128)(2,1)}), bf16[256,4,2048]{0,2,1:T(8,128)(2,1)}) %all-gather.18.cloned.1.call-update) | async-done | bytes 4194320 | tf_op jit(solution)/shard_map/all_gather | solution.py:16
  775.2 7.9 fusion.4
  783.1 0.0 all-gather.22.cloned.1.call-start
  783.1 125.0 %all-gather.20.cloned.1.call-done = bf16[2048,4,512]{0,2,1:T(8,128)(2,1)} async-done(((bf16[256,4,512]{0,2,1:T(8,128)(2,1)}), bf16[2048,4,512]{0,2,1:T(8,128)(2,1)}) %all-gather.20.cloned.1.call-update) | async-done | bytes 8388624 | tf_op jit(solution)/shard_map/all_gather | solution.py:29
  908.2 8.0 fusion.6
  916.2 0.0 all-gather.24.cloned.1.call-start
  916.3 123.2 %all-gather.22.cloned.1.call-done = bf16[2048,4,512]{0,2,1:T(8,128)(2,1)} async-done(((bf16[256,4,512]{0,2,1:T(8,128)(2,1)}), bf16[2048,4,512]{0,2,1:T(8,128)(2,1)}) %all-gather.22.cloned.1.call-update) | async-done | bytes 8388624 | tf_op jit(solution)/shard_map/all_gather | solution.py:29
  1039.5 5.7 fusion.11
  1045.2 0.8 fusion.34
  1046.1 0.5 all-gather.26.cloned.1.call-update
  1046.6 14.4 %all-gather.24.cloned.1.call-done = bf16[128,2,2048]{0,2,1:T(8,128)(2,1)} async-done(((bf16[128,2,512]{0,2,1:T(8,128)(2,1)}), bf16[128,2,2048]{0,2,1:T(8,128)(2,1)}) %all-gather.24.cloned.1.call-update) | async-done | bytes 1048592 | tf_op jit(solution)/shard_map/all_gather | solution.py:16
  1061.1 5.5 all-to-all-start
  1066.6 6.3 fusion.15
  1072.9 1.0 copy.20
  1073.8 27.3 %all-to-all-done = bf16[128,8,512]{0,2,1:T(8,128)(2,1)S(1)} async-done(((bf16[128,8,512]{0,2,1:T(8,128)(2,1)}), bf16[128,8,512]{0,2,1:T(8,128)(2,1)S(1)}, u32[]{:S(2)}, u32[]{:S(2)}) %all-to-all-start) | async-done | bytes 1048608 | tf_op jit(solution)/shard_map/all_to_all | solution.py:103
  1101.2 0.7 copy.16
  1101.9 0.5 reshape.81
  1102.4 22.7 %all-gather.26.cloned.1.call-done = bf16[1024,2,512]{0,2,1:T(8,128)(2,1)} async-done(((bf16[128,2,512]{0,2,1:T(8,128)(2,1)}), bf16[1024,2,512]{0,2,1:T(8,128)(2,1)}) %all-gather.26.cloned.1.call-update) | async-done | bytes 2097168 | tf_op jit(solution)/shard_map/all_gather | solution.py:107
  1125.1 2.9 multiply_convert_fusion
  1128.0 2.0 copy.19
  (29 shorter events, 0.4 us)
Async XLA Ops:
  7.2 28.3 %all-gather.10.cloned.1.call-start = ((), (), s32[]{:S(2)}) async-start(), calls=%async_computation.2 | async-start | bytes 2621440 | tf_op jit(solution)/shard_map/all_gather | solution.py:16
  9.2 0.8 copy-start.1
  10.0 315.7 %reduce-scatter.2.cloned.1.call-start = ((), (), s32[]{:S(2)}) async-start(), calls=%async_computation.3 | async-start | bytes 18874368 | tf_op jit(solution)/shard_map/reduce_scatter | solution.py:20
  45.3 442.7 %all-gather.16.cloned.1.call-start = ((), (), s32[]{:S(2)}) async-start(), calls=%async_computation.6 | async-start | bytes 5242880 | tf_op jit(solution)/shard_map/all_gather | solution.py:16
  325.7 42.7 %copy-start = (f32[256,4,512]{0,2,1:T(8,128)S(1)}, f32[256,4,512]{0,2,1:T(8,128)}, u32[]{:S(2)}) copy-start(f32[256,4,512]{0,2,1:T(8,128)} %reduce-scatter.2.cloned.1.call-done) | copy-start | bytes 6291460
  453.6 161.9 %all-gather.14.cloned.1.call-start = ((), (), s32[]{:S(2)}) async-start(), calls=%async_computation.5 | async-start | bytes 9437184 | tf_op jit(solution)/shard_map/all_gather | solution.py:29
  454.2 286.3 %all-gather.12.cloned.1.call-start = ((), (), s32[]{:S(2)}) async-start(), calls=%async_computation.4 | async-start | bytes 9437184 | tf_op jit(solution)/shard_map/all_gather | solution.py:29
  454.8 320.4 %all-gather.18.cloned.1.call-start = ((), (), s32[]{:S(2)}) async-start(), calls=%async_computation.7 | async-start | bytes 5242880 | tf_op jit(solution)/shard_map/all_gather | solution.py:16
  623.4 284.8 %all-gather.20.cloned.1.call-start = ((), (), s32[]{:S(2)}) async-start(), calls=%async_computation.8 | async-start | bytes 9437184 | tf_op jit(solution)/shard_map/all_gather | solution.py:29
  783.1 256.4 %all-gather.22.cloned.1.call-start = ((), (), s32[]{:S(2)}) async-start(), calls=%async_computation.9 | async-start | bytes 9437184 | tf_op jit(solution)/shard_map/all_gather | solution.py:29
  908.2 131.3 %copy-start.2 = (bf16[128,4,2048]{2,0,1:T(8,128)(2,1)S(1)}, bf16[128,4,2048]{2,0,1:T(8,128)(2,1)}, u32[]{:S(2)}) copy-start(bf16[128,4,2048]{2,0,1:T(8,128)(2,1)} %all-gather.10.cloned.1.call-done) | copy-start | bytes 6291460
  916.2 144.9 %all-gather.24.cloned.1.call-start = ((), (), s32[]{:S(2)}) async-start(), calls=%async_computation.10 | async-start | bytes 1310720 | tf_op jit(solution)/shard_map/all_gather | solution.py:16
  1046.1 79.0 %all-gather.26.cloned.1.call-start = ((), (), s32[]{:S(2)}) async-start(), calls=%async_computation.11 | async-start | bytes 2359296 | tf_op jit(solution)/shard_map/all_gather | solution.py:107
  1061.1 40.1 %all-to-all-start = ((bf16[128,8,512]{0,2,1:T(8,128)(2,1)}), bf16[128,8,512]{0,2,1:T(8,128)(2,1)S(1)}, u32[]{:S(2)}, u32[]{:S(2)}) async-start(bf16[128,8,512]{0,2,1:T(8,128)(2,1)} %bitcast.57), calls=%async_computation.1 | async-start | bytes 2097152 | tf_op jit(solution)/shard_map/all_to_all | solution.py:103
Sparse Core Ops, SparseCore 0:
  10.1 25.2 all-gather.9
  45.5 280.1 reduce-scatter.1
  453.7 34.2 all-gather.15
  490.5 124.9 all-gather.13
  617.4 123.1 all-gather.11
  742.5 32.6 all-gather.17
  783.2 124.9 all-gather.19
  916.3 123.1 all-gather.21
  1046.2 14.8 all-gather.23
  1063.5 61.5 all-gather.25
where the time goes:
time: 1140 us
  waiting for transfers between devices  932 us (82%)
  blocking collectives  120 us (11%)
  matrix products  54.2 us (5%)
  between operations  14.3 us (1%)
    all_gather x4, waiting for transfers between devices, shared_rows(): return lax.all_gather(piece, ('tok', 'grp'), axis=0, tiled=True)  493 us
    reduce_scatter x1, waiting for transfers between devices, token_sums(): lax.psum_scatter(maker(jnp.int32(0), rows * lax.axis_size(('tok', 'grp'))...  280 us
    psum x3, blocking collectives, shared_total(): return lax.psum(vector, ('tok', 'out', 'grp'))  120 us
    all_gather x4, waiting for transfers between devices, spread(): return lax.all_gather(piece, 'out', axis=2, tiled=True)  108 us
    all_to_all x1, waiting for transfers between devices, local(): lax.all_to_all(acts_whole, ('tok', 'grp'), split_axis=1, concat_axis=0, t...  27.3 us
    dot_general x3, matrix products, multiply(): jnp.einsum('rkj,jkc->rkc', row_band, column_band, preferred_element_type=...  23.8 us
  transfers between devices with their start and end apart: 11, of which 11 were waited for; matrix products, arithmetic and copies ran while one was open for 1% of the time, Pallas kernels for 0%

commit v1 on v0

--- a/solution.py
+++ b/solution.py
@@ -111,6 +111,78 @@
     return (update, input_grad)
 
 
+def token_space_whiten(sides, cols):
+    tokens, block = sides.shape
+    gram = jnp.einsum("tc,uc->tu", sides, sides, preferred_element_type=jnp.float32) / tokens
+    ray_0 = jnp.sum(sides.astype(jnp.float32), axis=1)
+    ray_1 = jnp.sum(gram * ray_0[None, :], axis=1) + DAMPING * ray_0
+    ray_2 = jnp.sum(gram * ray_1[None, :], axis=1) + DAMPING * ray_1
+    dots = [
+        jnp.sum(ray_0 * ray_0),
+        jnp.sum(ray_0 * ray_1),
+        jnp.sum(ray_1 * ray_1),
+        jnp.sum(ray_1 * ray_2),
+        jnp.sum(ray_2 * ray_2),
+    ]
+
+    def moment(power):
+        total = DAMPING**power * block
+        for i in range(power):
+            total = total + DAMPING ** (power - 1 - i) * dots[i] / tokens
+        return total
+
+    scale = moment(2 * POWER - 1) / moment(2 * POWER - 2)
+    low = (gram / scale).astype(jnp.bfloat16)
+    shift = DAMPING / scale
+
+    def apply(value):
+        product = jnp.einsum(
+            "tu,uc->tc", low, value.astype(jnp.bfloat16), preferred_element_type=jnp.float32
+        )
+        return product + shift * value
+
+    def first(value):
+        return (3.0 * value - apply(value)) / 2.0
+
+    head = first(cols.astype(jnp.float32))
+    tail = first(first(apply(head)))
+    return ((3.0 * head - tail) / 2.0 / jnp.sqrt(scale)).astype(jnp.bfloat16)
+
+
+def planes(activations, out_grads, weight):
+    tok_dev, blocks, width = activations.shape
+    count = 2 * blocks
+    tok, grp, out = (lax.axis_size(name) for name in ("tok", "grp", "out"))
+    block = width * out
+    token_count = tok_dev * tok * grp
+    part = width // grp
+    local_sides = jnp.concatenate([activations, out_grads], axis=1)
+    pieces = jnp.swapaxes(local_sides, 0, 1)
+    mine = lax.all_to_all(pieces, "tok", split_axis=0, concat_axis=0, tiled=True)
+    mine = mine.reshape(tok * tok_dev, width)
+    whole = lax.all_gather(mine, ("grp", "out"), axis=0, tiled=False)
+    whole = whole.reshape(grp, out, tok * tok_dev, width)
+    sides = jnp.transpose(whole, (0, 2, 1, 3)).reshape(token_count, block)
+    start = lax.axis_index("out") * width + lax.axis_index("grp") * part
+    cols = lax.dynamic_slice_in_dim(sides, start, part, 1)
+    whitened = token_space_whiten(sides, cols)
+    spread_low = lax.all_gather(whitened, ("tok", "grp"), axis=0, tiled=False)
+    spread_low = spread_low.reshape(count, grp, token_count, part)
+    grads_low = spread_low[blocks:]
+    row = lax.axis_index(("tok", "grp"))
+    own = lax.dynamic_index_in_dim(spread_low, row // out, 0, keepdims=False)
+    owner = lax.rem(row, out) == lax.axis_index("out")
+    acts_low = lax.psum(jnp.where(owner, own, jnp.zeros_like(own)), "out")
+    update = jnp.einsum("yta,bxtc->yabxc", acts_low, grads_low, preferred_element_type=jnp.float32)
+    update = (update / math.sqrt(token_count)).astype(jnp.bfloat16).reshape(width, blocks, width)
+    grads_whole = spread(out_grads)
+    weight_rows = weight.reshape(blocks, width, blocks, block)
+    input_grad = jnp.einsum(
+        "tjq,bcjq->tbc", grads_whole, weight_rows, preferred_element_type=jnp.float32
+    ).astype(jnp.bfloat16)
+    return (update, input_grad)
+
+
 def solution(mesh):
     in_specs = (
         P(("tok", "grp"), None, "out"),
@@ -118,4 +190,11 @@
         P(None, "out", None),
     )
     out_specs = (P(("tok", "grp"), None, "out"), P(("tok", "grp"), None, "out"))
-    return jax.shard_map(local, mesh=mesh, in_specs=in_specs, out_specs=out_specs, check_vma=False)
+
+    def body(activations, out_grads, weight):
+        blocks = activations.shape[1]
+        tok, grp, out = (mesh.shape[name] for name in ("tok", "grp", "out"))
+        fits = tok == 2 * blocks and tok * grp == blocks * out
+        return (planes if fits else local)(activations, out_grads, weight)
+
+    return jax.shard_map(body, mesh=mesh, in_specs=in_specs, out_specs=out_specs, check_vma=False)

time: 1140 us -> 238 us (0.21)
  waiting for transfers between devices: 932 us -> 154 us
  blocking collectives: 120 us -> 20.7 us
  matrix products: 54.2 us -> 19.4 us
    all_gather x5 -> x2, waiting for transfers between devices: 515 us -> 108 us  [the longest x1 72 us: planes(): spread_low = lax.all_gather(whitened, ('tok', 'grp'), axis=0, tiled=False)]
    reduce_scatter x1 -> x0, waiting for transfers between devices: 280 us -> none  [token_sums(): lax.psum_scatter(maker(jnp.int32(0), rows * lax.axis_size(('tok', 'grp'))...]
    psum x3 -> x0, blocking collectives: 120 us -> none  [shared_total(): return lax.psum(vector, ('tok', 'out', 'grp'))]
    all_gather x4 -> x1, waiting for transfers between devices: 108 us -> 14.5 us  [spread(): return lax.all_gather(piece, 'out', axis=2, tiled=True)]
    dot_general x10 -> x7, matrix products: 54.2 us -> 19.4 us  [the longest x1 6.75 us: planes(): jnp.einsum('tjq,bcjq->tbc', grads_whole, weight_rows, preferred_element_t...]
    psum x0 -> x1, waiting for transfers between devices: none -> 31.2 us  [planes(): acts_low = lax.psum(jnp.where(owner, own, jnp.zeros_like(own)), 'out')]
    all_to_all x1 -> x0, waiting for transfers between devices: 27.3 us -> none  [local(): lax.all_to_all(acts_whole, ('tok', 'grp'), split_axis=1, concat_axis=0, t...]
    all_to_all x0 -> x1, blocking collectives: none -> 20.7 us  [planes(): lax.all_to_all(pieces, 'tok', split_axis=0, concat_axis=0, tiled=True)]
  transfers between devices with their start and end apart: 11 -> 4, of which waited for: 11 -> 4; matrix products, arithmetic and copies ran while one was open for 1% -> 5% of each run, Pallas kernels for 0% -> 0%
where the time goes in v1:
time: 238 us; the launch traced here: 237 us
  waiting for transfers between devices  154 us (65%)
  blocking collectives  20.7 us (9%)
  between operations  19.6 us (8%)
  matrix products  19.4 us (8%)
  local copies, waits for them, and re-layouts  14.6 us (6%)
  other arithmetic  8.42 us (4%)
    all_gather x1, waiting for transfers between devices, planes(): spread_low = lax.all_gather(whitened, ('tok', 'grp'), axis=0, tiled=False)  72 us
    all_gather x1, waiting for transfers between devices, planes(): whole = lax.all_gather(mine, ('grp', 'out'), axis=0, tiled=False)  35.8 us
    psum x1, waiting for transfers between devices, planes(): acts_low = lax.psum(jnp.where(owner, own, jnp.zeros_like(own)), 'out')  31.2 us
    all_to_all x1, blocking collectives, planes(): lax.all_to_all(pieces, 'tok', split_axis=0, concat_axis=0, tiled=True)  20.7 us
    all_gather x1, waiting for transfers between devices, spread(): return lax.all_gather(piece, 'out', axis=2, tiled=True)  14.5 us
    unnamed x18, local copies, waits for them, and re-layouts  9.98 us
    dot_general x1, matrix products, planes(): jnp.einsum('tjq,bcjq->tbc', grads_whole, weight_rows, preferred_element_t...  6.75 us
    dot_general x4, matrix products, apply(): jnp.einsum('tu,uc->tc', low, value.astype(jnp.bfloat16), preferred_elemen...  5.66 us
  transfers between devices with their start and end apart: 4, of which 4 were waited for; matrix products, arithmetic and copies ran while one was open for 5% of the time, Pallas kernels for 0%

profile of v1, /device:TPU:0, one launch (start us, length us, event | category | flops | bytes accessed | tf_op | source)
XLA Modules:
  0.0 237.2 jit_solution(17187461038520449811)
XLA Ops:
  7.2 0.0 all-gather.5.cloned.1.call-start
  7.2 1.0 copy.28
  8.2 0.0 copy-start.4
  8.2 1.1 copy.27
  9.3 20.7 %all_to_all.5 = bf16[4,128,512]{2,1,0:T(8,128)(2,1)} all-to-all(bf16[4,128,512]{2,1,0:T(8,128)(2,1)S(1)} %maximum_bitcast_fusion), channel_id=1, replica_groups=mesh['tok'=4,'out'=4,'grp'=2] {'tok'}, dimensions={0} | all-to-all | bytes 1048576 | tf_op jit(solution)/shard_map/all_to_all | solution.py:161
  30.1 0.0 all-gather.5.cloned.1.call-update
  30.1 0.0 all-gather.9.cloned.1.call-start
  30.2 35.8 %all-gather.5.cloned.1.call-done = bf16[8,512,512]{2,1,0:T(8,128)(2,1)} async-done(((bf16[1,512,512]{2,1,0:T(8,128)(2,1)}), bf16[8,512,512]{2,1,0:T(8,128)(2,1)}) %all-gather.5.cloned.1.call-update) | async-done | bytes 4194320 | tf_op jit(solution)/shard_map/all_gather | solution.py:163
  66.0 0.0 copy-start.1
  66.0 3.0 %convert_reduce_fusion = f32[2,512]{1,0:T(2,128)S(1)} fusion(bf16[2,512,4,512]{3,1,2,0:T(8,128)(2,1)} %bitcast.45), kind=kLoop, calls=%fused_computation.3 | loop fusion | flops 4193280 | bytes 4198400 | tf_op jit(solution)/shard_map/reduce_sum | solution.py:117
  68.9 0.5 copy-done.1
  69.4 3.2 %copy.29 = bf16[2,512,4,512]{3,2,1,0:T(4,128)(2,1)S(1)} copy(bf16[2,512,4,512]{3,1,2,0:T(8,128)(2,1)S(1)} %bitcast.46) | data formatting | bytes 8388608 | tf_op jit(solution)/shard_map/transpose | solution.py:165
  72.6 0.0 copy-done.4
  72.7 0.6 multiply_reduce_fusion.6
  73.3 1.4 copy.42
  74.7 0.0 copy-start.2
  74.7 4.5 %multiply_reduce_fusion.1 = (f32[1024]{0:T(1024)S(1)}, f32[1024,1024]{0,1:T(8,128)S(1)}) fusion(f32[1024]{0:T(1024)S(1)} %broadcast_multiply_fusion.1, bf16[1024,2048]{1,0:T(8,128)(2,1)S(1)} %bitcast.48), kind=kOutput, calls=%fused_computation.6 | convolution fusion | flops 4297063424 | bytes 8396800 | tf_op jit(solution)/shard_map/tc,uc->tu/dot_general | solution.py:116
  79.2 0.0 copy-done.2
  79.2 0.0 copy-start
  79.3 1.9 copy-done
  81.2 0.3 multiply_reduce_fusion
  81.5 0.6 multiply_reduce_fusion.2
  87.7 2.8 %divide_convert_fusion = bf16[1024,1024]{0,1:T(8,128)(2,1)S(1)} fusion(f32[1024,1024]{0,1:T(8,128)} %copy-done, f32[]{:T(128)S(6)} %div.88), kind=kLoop, calls=%fused_computation.4 | loop fusion | flops 3145728 | bytes 6291460 | tf_op jit(solution)/shard_map/convert_element_type | solution.py:135
  90.6 2.1 fusion.8
  92.8 0.8 convolution_add_fusion.2
  93.6 0.9 fusion.7
  94.5 1.8 fusion.10
  96.3 0.0 all-gather.9.cloned.1.call-update
  96.3 0.0 all-gather.7.cloned.1.call-start
  96.4 0.7 all-gather.7.cloned.1.call-update
  97.1 0.0 all-reduce.2.cloned.1.call-start
  97.1 72.0 %all-gather.9.cloned.1.call-done = bf16[8192,256]{1,0:T(8,128)(2,1)} async-done(((bf16[1024,256]{1,0:T(8,128)(2,1)}), bf16[8192,256]{1,0:T(8,128)(2,1)}) %all-gather.9.cloned.1.call-update) | async-done | bytes 4194320 | tf_op jit(solution)/shard_map/all_gather | solution.py:169
  169.1 1.3 constant_dynamic-slice_fusion
  170.4 0.5 copy.40
  170.9 1.0 select_bitcast_fusion
  172.0 0.0 all-reduce.2.cloned.1.call-update
  172.0 14.5 %all-gather.7.cloned.1.call-done = bf16[128,2,2048]{2,0,1:T(8,128)(2,1)} async-done(((bf16[128,2,512]{2,0,1:T(8,128)(2,1)}), bf16[128,2,2048]{2,0,1:T(8,128)(2,1)}) %all-gather.7.cloned.1.call-update) | async-done | bytes 1048592 | tf_op jit(solution)/shard_map/all_gather | solution.py:16
  186.5 0.0 copy-start.3
  186.5 6.7 %fusion.14 = bf16[128,2,512]{2,0,1:T(8,128)(2,1)S(1)} fusion(bf16[2,64,2,8,2048]{4,3,2,1,0:T(8,128)(2,1)} %bitcast.57, bf16[128,2,2048]{2,0,1:T(8,128)(2,1)} %all-gather.7.cloned.1.call-done), kind=kOutput, calls=%fused_computation.23 | convolution fusion | flops 1073872896 | bytes 9699328 | tf_op jit(solution)/shard_map/tjq,bcjq->tbc/dot_general | solution.py:180
  193.3 1.0 copy.35
  194.2 0.0 copy-done.3
  194.2 0.1 slice.9
  194.4 31.2 %all-reduce.2.cloned.1.call-done = bf16[2,1024,256]{1,2,0:T(8,128)(2,1)} async-done(((bf16[2,1024,256]{1,2,0:T(8,128)(2,1)}), bf16[2,1024,256]{1,2,0:T(8,128)(2,1)}) %all-reduce.2.cloned.1.call-update) | async-done | bytes 1048592 | tf_op jit(solution)/shard_map/psum | solution.py:175
  225.6 2.5 %multiply_convert_fusion = bf16[2,256,2,2,256]{4,1,3,2,0:T(8,128)(2,1)S(1)} fusion(bf16[2,2,1024,256,1]{3,2,1,0,4:T(8,128)(2,1)S(1)} %bitcast.51, bf16[2,1024,256]{1,2,0:T(8,128)(2,1)} %all-reduce.2.cloned.1.call-done), kind=kOutput, calls=%fused_computation.7 | convolution fusion | flops 1074790400 | bytes 4194304 | tf_op jit(solution)/shard_map/yta,bxtc->yabxc/dot_general | solution.py:176
  228.1 1.1 copy.38
  229.2 1.5 reshape.68
  (4 shorter events, 0.1 us)
Async XLA Ops:
  7.2 58.8 %all-gather.5.cloned.1.call-start = ((), (), s32[]{:S(2)}) async-start(), calls=%async_computation.1 | async-start | bytes 4718592 | tf_op jit(solution)/shard_map/all_gather | solution.py:163
  8.2 64.5 %copy-start.4 = (bf16[128,2,512]{2,0,1:T(8,128)(2,1)}, bf16[128,2,512]{2,0,1:T(8,128)(2,1)S(1)}, u32[]{:S(2)}) copy-start(bf16[128,2,512]{2,0,1:T(8,128)(2,1)S(1)} %copy.28) | copy-start | bytes 786436
  30.1 139.0 %all-gather.9.cloned.1.call-start = ((), (), s32[]{:S(2)}) async-start(), calls=%async_computation.4 | async-start | bytes 4718592 | tf_op jit(solution)/shard_map/all_gather | solution.py:169
  66.0 3.4 %copy-start.1 = (bf16[8,512,512]{2,1,0:T(8,128)(2,1)S(1)}, bf16[8,512,512]{2,1,0:T(8,128)(2,1)}, u32[]{:S(2)}) copy-start(bf16[8,512,512]{2,1,0:T(8,128)(2,1)} %all-gather.5.cloned.1.call-done) | copy-start | bytes 12582916
  74.7 4.6 %copy-start.2 = (bf16[128,8,4,512]{3,1,2,0:T(8,128)(2,1)}, bf16[128,8,4,512]{3,1,2,0:T(8,128)(2,1)S(1)}, u32[]{:S(2)}) copy-start(bf16[128,8,4,512]{3,1,2,0:T(8,128)(2,1)S(1)} %copy.42) | copy-start | bytes 12582916
  79.2 2.0 copy-start
  96.3 90.2 %all-gather.7.cloned.1.call-start = ((), (), s32[]{:S(2)}) async-start(), calls=%async_computation.3 | async-start | bytes 1310720 | tf_op jit(solution)/shard_map/all_gather | solution.py:16
  97.1 128.6 %all-reduce.2.cloned.1.call-start = ((), (), s32[]{:S(2)}) async-start(), calls=%async_computation.2 | async-start | bytes 2097152 | tf_op jit(solution)/shard_map/psum | solution.py:175
  186.5 7.7 %copy-start.3 = (bf16[8192,256]{1,0:T(8,128)(2,1)S(1)}, bf16[8192,256]{1,0:T(8,128)(2,1)}, u32[]{:S(2)}) copy-start(bf16[8192,256]{1,0:T(8,128)(2,1)} %all-gather.9.cloned.1.call-done) | copy-start | bytes 12582916
Sparse Core Ops, SparseCore 0:
  30.2 35.6 all-gather.4
  96.4 72.6 all-gather.8
  171.2 15.2 all-gather.6
  189.3 36.2 all-reduce.1

commit v2 on v1

--- a/solution.py
+++ b/solution.py
@@ -3,6 +3,8 @@
 import jax
 import jax.numpy as jnp
 from jax import lax
+from jax.experimental import pallas as pl
+from jax.experimental.pallas import tpu as pltpu
 from jax.sharding import PartitionSpec as P
 
 POWER = 3
@@ -111,6 +113,297 @@
     return (update, input_grad)
 
 
+MESH = pl.DeviceIdType.MESH
+HOPS = (0, 1, 3, 2)
+CHUNKS = 4
+
+
+def greet(peers):
+    barrier = pltpu.get_barrier_semaphore()
+    for peer in peers:
+        pl.semaphore_signal(barrier, inc=1, device_id=peer, device_id_type=MESH)
+    pl.semaphore_wait(barrier, len(peers))
+
+
+def remote(src, dst, send, recv, peer):
+    return pltpu.make_async_remote_copy(
+        src_ref=src, dst_ref=dst, send_sem=send, recv_sem=recv, device_id=peer, device_id_type=MESH
+    )
+
+
+def neighbours():
+    z, o, y = lax.axis_index("tok"), lax.axis_index("out"), lax.axis_index("grp")
+    ox = lax.rem(o + 2, 4)
+    oc = o + 1 - 2 * lax.rem(o, 2)
+    at = lambda a, b, c: {"tok": a, "out": b, "grp": c}
+    zs = [lax.rem(z + j, 4) for j in range(4)]
+    peers = [at(zs[j], o, y) for j in (1, 2, 3)]
+    return z, o, y, ox, oc, zs, peers, at(z, o, 1 - y), at(z, ox, y), at(z, oc, y)
+
+
+def collect_kernel(pieces, sides, grads, send, recv, grads_recv, local):
+    z, o, y, ox, oc, zs, z_peers, y_peer, x_peer, c_peer = neighbours()
+    rows, width = pieces.shape[1:]
+    count = [0]
+
+    def tile(oi, yi, zi):
+        return sides.at[
+            pl.ds(pl.multiple_of((yi * 4 + zi) * rows, rows), rows),
+            pl.ds(pl.multiple_of(oi * width, width), width),
+        ]
+
+    def band(oi):
+        return grads.at[:, :, pl.ds(pl.multiple_of(oi * width, width), width)]
+
+    sent = []
+
+    def push(src, dst, sem, peer):
+        copy = remote(src, dst, send.at[count[0]], sem, peer)
+        count[0] += 1
+        copy.start()
+        sent.append(copy)
+
+    def sem_of(oi, yi, zi):
+        return recv.at[oi * 8 + yi * 4 + zi]
+
+    def arrived(oi, yi, zi):
+        ref = tile(oi, yi, zi)
+        remote(ref, ref, send.at[0], sem_of(oi, yi, zi), c_peer).wait_recv()
+        return ref
+
+    def forward(src, oi, yi, zi, peers):
+        for peer in peers:
+            push(src, tile(oi, yi, zi), sem_of(oi, yi, zi), peer)
+
+    greet(z_peers + [y_peer, x_peer, c_peer])
+    for j in (1, 3, 2):
+        push(pieces.at[zs[j]], tile(o, y, z), sem_of(o, y, z), z_peers[j - 1])
+    own = pltpu.make_async_copy(pieces.at[z], tile(o, y, z), local.at[0])
+    own.start()
+    forward(pieces.at[z], o, y, z, (y_peer, x_peer, c_peer))
+    low = pieces.at[1:3]
+    own_grads = pltpu.make_async_copy(low, band(o), local.at[1])
+    own_grads.start()
+    for peer in (x_peer, c_peer):
+        push(low, band(o), grads_recv.at[o], peer)
+    for j in (1, 3, 2):
+        forward(arrived(o, y, zs[j]), o, y, zs[j], (y_peer, x_peer, c_peer))
+    for step, j in enumerate(HOPS):
+        ref = arrived(o, 1 - y, zs[j])
+        forward(ref, o, 1 - y, zs[j], (x_peer, c_peer) if step % 2 == 0 else (c_peer,))
+        ref = arrived(ox, y, zs[j])
+        forward(ref, ox, y, zs[j], (y_peer, c_peer) if step % 2 == 1 else (c_peer,))
+    ref = band(ox)
+    remote(ref, ref, send.at[0], grads_recv.at[ox], c_peer).wait_recv()
+    push(ref, ref, grads_recv.at[ox], c_peer)
+    for j in HOPS:
+        forward(arrived(ox, 1 - y, zs[j]), ox, 1 - y, zs[j], (c_peer,))
+    oxc = lax.rem(oc + 2, 4)
+    for oi in (oc, oxc):
+        for yi in (y, 1 - y):
+            for j in HOPS:
+                arrived(oi, yi, zs[j])
+        ref = band(oi)
+        remote(ref, ref, send.at[0], grads_recv.at[oi], c_peer).wait_recv()
+    own.wait()
+    own_grads.wait()
+    for copy in sent:
+        copy.wait_send()
+
+
+def collect(pieces):
+    count, rows, width = pieces.shape
+    sends = 3 + 3 * 4 + 3 * 4 + 4 + 3 + 4
+    return pl.pallas_call(
+        collect_kernel,
+        out_shape=(
+            jax.ShapeDtypeStruct((rows * 8, width * 4), pieces.dtype),
+            jax.ShapeDtypeStruct((count // 2, rows, width * 4), pieces.dtype),
+        ),
+        in_specs=[pl.BlockSpec(memory_space=pltpu.VMEM)],
+        out_specs=(pl.BlockSpec(memory_space=pltpu.VMEM), pl.BlockSpec(memory_space=pltpu.VMEM)),
+        scratch_shapes=[
+            pltpu.SemaphoreType.DMA((sends,)),
+            pltpu.SemaphoreType.DMA((32,)),
+            pltpu.SemaphoreType.DMA((4,)),
+            pltpu.SemaphoreType.DMA((2,)),
+        ],
+        compiler_params=pltpu.CompilerParams(collective_id=0, has_side_effects=True),
+        name="collect",
+    )(pieces)
+
+
+def deliver_kernel(low, grads, acts, g_send, y_send, g_recv, y_recv, a_send, a_recv, hub_send, hub_recv, local):
+    z, o, y, ox, oc, zs, z_peers, y_peer, x_peer, c_peer = neighbours()
+    tokens, part = low.shape
+    rows = tokens // CHUNKS
+    oxc = lax.rem(oc + 2, 4)
+    row = 2 * z + y
+    hub = lax.rem(row, 4)
+    is_grad = (z == 1) | (z == 2)
+    mine = z - 1
+    base = (z // 3) * 2
+    goal_z, goal_y = base + o // 2, lax.rem(o, 2)
+    stays = (goal_z == z) & (goal_y == y)
+    goal = {"tok": goal_z, "out": o, "grp": goal_y}
+    source_z = (row // 4) * 3
+    greet_all = z_peers + [y_peer, x_peer, c_peer] + [
+        {"tok": zs[j], "out": o, "grp": 1 - y} for j in (1, 2, 3)
+    ]
+    greet(greet_all)
+
+    def span(c):
+        return pl.ds(c * rows, rows)
+
+    def piece(c):
+        return low.at[span(c), :]
+
+    def half(yi):
+        return pl.ds(pl.multiple_of(yi * part, part), part)
+
+    def g_tile(b, yi, c):
+        return grads.at[b, span(c), half(yi)]
+
+    def a_tile(yi, c):
+        return acts.at[span(c), half(yi)]
+
+    def own_grad(c):
+        return pltpu.make_async_copy(piece(c), g_tile(mine, y, c), local.at[c])
+
+    def own_act(c):
+        return pltpu.make_async_copy(piece(c), a_tile(y, c), local.at[c])
+
+    def to_plane(c, j):
+        return remote(
+            piece(c), g_tile(mine, y, c), g_send.at[c * 3 + j - 1], g_recv.at[mine * CHUNKS + c], z_peers[j - 1]
+        )
+
+    def y_copy(src, b, c):
+        return remote(
+            src, g_tile(b, y, c), y_send.at[b * CHUNKS + c], y_recv.at[b * CHUNKS + c], y_peer
+        )
+
+    def to_hub(c):
+        return remote(piece(c), a_tile(y, c), a_send.at[c], a_recv.at[y * CHUNKS + c], goal)
+
+    def from_hub(yi, c, way, peer):
+        ref = a_tile(yi, c)
+        return remote(
+            ref, ref, hub_send.at[way * 2 * CHUNKS + yi * CHUNKS + c], hub_recv.at[yi * CHUNKS + c], peer
+        )
+
+    for c in range(CHUNKS):
+
+        @pl.when(is_grad)
+        def _():
+            for j in (1, 3, 2):
+                to_plane(c, j).start()
+            y_copy(piece(c), mine, c).start()
+            own_grad(c).start()
+
+        @pl.when(jnp.logical_not(is_grad) & stays)
+        def _():
+            own_act(c).start()
+
+        @pl.when(jnp.logical_not(is_grad) & jnp.logical_not(stays))
+        def _():
+            to_hub(c).start()
+
+    def hub_step(c):
+        for yi in range(2):
+            here = (source_z == z) & (y == yi)
+
+            @pl.when((o == hub) & here)
+            def _():
+                own_act(c).wait()
+
+            @pl.when((o == hub) & jnp.logical_not(here))
+            def _():
+                ref = a_tile(yi, c)
+                remote(ref, ref, a_send.at[0], a_recv.at[yi * CHUNKS + c], c_peer).wait_recv()
+
+            @pl.when(o == hub)
+            def _():
+                from_hub(yi, c, 0, x_peer).start()
+                from_hub(yi, c, 1, c_peer).start()
+
+    def relay_step(c):
+        for yi in range(2):
+
+            @pl.when(o != hub)
+            def _():
+                from_hub(yi, c, 0, c_peer).wait_recv()
+
+            @pl.when(ox == hub)
+            def _():
+                from_hub(yi, c, 1, c_peer).start()
+
+    for c in range(CHUNKS):
+        for b in range(2):
+
+            @pl.when(z != b + 1)
+            def _():
+                ref = g_tile(b, y, c)
+                remote(ref, ref, g_send.at[0], g_recv.at[b * CHUNKS + c], c_peer).wait_recv()
+                y_copy(ref, b, c).start()
+
+        hub_step(c)
+    for c in range(CHUNKS):
+        relay_step(c)
+    for c in range(CHUNKS):
+        for b in range(2):
+            ref = g_tile(b, 1 - y, c)
+            remote(ref, ref, y_send.at[0], y_recv.at[b * CHUNKS + c], c_peer).wait_recv()
+            y_copy(g_tile(b, y, c), b, c).wait_send()
+
+        @pl.when(is_grad)
+        def _():
+            for j in (1, 3, 2):
+                to_plane(c, j).wait_send()
+            own_grad(c).wait()
+
+        @pl.when(jnp.logical_not(is_grad) & jnp.logical_not(stays))
+        def _():
+            to_hub(c).wait_send()
+
+        for yi in range(2):
+
+            @pl.when(o == hub)
+            def _():
+                from_hub(yi, c, 0, x_peer).wait_send()
+
+            @pl.when((o == hub) | (ox == hub))
+            def _():
+                from_hub(yi, c, 1, c_peer).wait_send()
+
+
+def deliver(low):
+    tokens, part = low.shape
+    dma = pltpu.SemaphoreType.DMA
+    return pl.pallas_call(
+        deliver_kernel,
+        out_shape=(
+            jax.ShapeDtypeStruct((2, tokens, 2 * part), low.dtype),
+            jax.ShapeDtypeStruct((tokens, 2 * part), low.dtype),
+        ),
+        in_specs=[pl.BlockSpec(memory_space=pltpu.VMEM)],
+        out_specs=(pl.BlockSpec(memory_space=pltpu.VMEM), pl.BlockSpec(memory_space=pltpu.VMEM)),
+        scratch_shapes=[
+            dma((3 * CHUNKS,)),
+            dma((2 * CHUNKS,)),
+            dma((2 * CHUNKS,)),
+            dma((2 * CHUNKS,)),
+            dma((CHUNKS,)),
+            dma((2 * CHUNKS,)),
+            dma((4 * CHUNKS,)),
+            dma((2 * CHUNKS,)),
+            dma((CHUNKS,)),
+        ],
+        compiler_params=pltpu.CompilerParams(collective_id=1, has_side_effects=True),
+        name="deliver",
+    )(low)
+
+
 def token_space_whiten(sides, cols):
     tokens, block = sides.shape
     gram = jnp.einsum("tc,uc->tu", sides, sides, preferred_element_type=jnp.float32) / tokens
@@ -151,34 +444,19 @@
 
 def planes(activations, out_grads, weight):
     tok_dev, blocks, width = activations.shape
-    count = 2 * blocks
-    tok, grp, out = (lax.axis_size(name) for name in ("tok", "grp", "out"))
-    block = width * out
-    token_count = tok_dev * tok * grp
-    part = width // grp
-    local_sides = jnp.concatenate([activations, out_grads], axis=1)
-    pieces = jnp.swapaxes(local_sides, 0, 1)
-    mine = lax.all_to_all(pieces, "tok", split_axis=0, concat_axis=0, tiled=True)
-    mine = mine.reshape(tok * tok_dev, width)
-    whole = lax.all_gather(mine, ("grp", "out"), axis=0, tiled=False)
-    whole = whole.reshape(grp, out, tok * tok_dev, width)
-    sides = jnp.transpose(whole, (0, 2, 1, 3)).reshape(token_count, block)
+    block = width * lax.axis_size("out")
+    part = width // lax.axis_size("grp")
+    token_count = tok_dev * lax.axis_size(("tok", "grp"))
+    pieces = jnp.stack([activations[:, 0], out_grads[:, 0], out_grads[:, 1], activations[:, 1]])
+    sides, grads_whole = collect(pieces)
     start = lax.axis_index("out") * width + lax.axis_index("grp") * part
     cols = lax.dynamic_slice_in_dim(sides, start, part, 1)
-    whitened = token_space_whiten(sides, cols)
-    spread_low = lax.all_gather(whitened, ("tok", "grp"), axis=0, tiled=False)
-    spread_low = spread_low.reshape(count, grp, token_count, part)
-    grads_low = spread_low[blocks:]
-    row = lax.axis_index(("tok", "grp"))
-    own = lax.dynamic_index_in_dim(spread_low, row // out, 0, keepdims=False)
-    owner = lax.rem(row, out) == lax.axis_index("out")
-    acts_low = lax.psum(jnp.where(owner, own, jnp.zeros_like(own)), "out")
-    update = jnp.einsum("yta,bxtc->yabxc", acts_low, grads_low, preferred_element_type=jnp.float32)
-    update = (update / math.sqrt(token_count)).astype(jnp.bfloat16).reshape(width, blocks, width)
-    grads_whole = spread(out_grads)
+    grads_low, acts_low = deliver(token_space_whiten(sides, cols))
+    update = jnp.einsum("ta,btc->abc", acts_low, grads_low, preferred_element_type=jnp.float32)
+    update = (update / math.sqrt(token_count)).astype(jnp.bfloat16)
     weight_rows = weight.reshape(blocks, width, blocks, block)
     input_grad = jnp.einsum(
-        "tjq,bcjq->tbc", grads_whole, weight_rows, preferred_element_type=jnp.float32
+        "jtq,bcjq->tbc", grads_whole, weight_rows, preferred_element_type=jnp.float32
     ).astype(jnp.bfloat16)
     return (update, input_grad)
 
@@ -194,7 +472,7 @@
     def body(activations, out_grads, weight):
         blocks = activations.shape[1]
         tok, grp, out = (mesh.shape[name] for name in ("tok", "grp", "out"))
-        fits = tok == 2 * blocks and tok * grp == blocks * out
+        fits = (blocks, tok, grp, out) == (2, 4, 2, 4)
         return (planes if fits else local)(activations, out_grads, weight)
 
     return jax.shard_map(body, mesh=mesh, in_specs=in_specs, out_specs=out_specs, check_vma=False)

time: 238 us -> 111 us (0.47)
  waiting for transfers between devices: 154 us -> 0 us
  Pallas kernels: 0 us -> 70.7 us
  blocking collectives: 20.7 us -> 0 us
  between operations: 19.6 us -> 6.33 us
  local copies, waits for them, and re-layouts: 14.6 us -> 8.08 us
  other arithmetic: 8.42 us -> 5.24 us
    all_gather x3 -> x0, waiting for transfers between devices: 122 us -> none  [the longest x1 72 us: planes(): spread_low = lax.all_gather(whitened, ('tok', 'grp'), axis=0, tiled=False)]
    pallas_call x0 -> x2, Pallas kernels: none -> 70.7 us  [the longest x1 36 us: deliver(): pl.pallas_call(deliver_kernel, out_shape=(jax.ShapeDtypeStruct((2, tokens...]
    psum x1 -> x0, waiting for transfers between devices: 31.2 us -> none  [planes(): acts_low = lax.psum(jnp.where(owner, own, jnp.zeros_like(own)), 'out')]
    all_to_all x1 -> x0, blocking collectives: 20.7 us -> none  [planes(): lax.all_to_all(pieces, 'tok', split_axis=0, concat_axis=0, tiled=True)]
    unnamed x18 -> x6, local copies, waits for them, and re-layouts: 9.98 us -> 4.98 us
    transpose x1 -> x0, local copies, waits for them, and re-layouts: 3.24 us -> none  [planes(): sides = jnp.transpose(whole, (0, 2, 1, 3)).reshape(token_count, block)]
    slice x1 -> x2, local copies, waits for them, and re-layouts: 0.14 us -> 3.03 us  [the longest x1 1.53 us: planes(): out_grads[:, 0]]
  transfers between devices with their start and end apart: 4 -> 0, of which waited for: 4 -> 0; matrix products, arithmetic and copies ran while one was open for 5% -> 0% of each run, Pallas kernels for 0% -> 0%
where the time goes in v2:
time: 111 us; the launch traced here: 110 us
  Pallas kernels  70.7 us (64%)
  matrix products  19.9 us (18%)
  local copies, waits for them, and re-layouts  8.08 us (7%)
  between operations  6.33 us (6%)
  other arithmetic  5.24 us (5%)
    pallas_call x1, Pallas kernels, deliver(): pl.pallas_call(deliver_kernel, out_shape=(jax.ShapeDtypeStruct((2, tokens...  36 us
    pallas_call x1, Pallas kernels, collect(): pl.pallas_call(collect_kernel, out_shape=(jax.ShapeDtypeStruct((rows * 8,...  34.7 us
    dot_general x1, matrix products, planes(): jnp.einsum('jtq,bcjq->tbc', grads_whole, weight_rows, preferred_element_t...  6.75 us
    dot_general x4, matrix products, apply(): jnp.einsum('tu,uc->tc', low, value.astype(jnp.bfloat16), preferred_elemen...  5.48 us
    unnamed x6, local copies, waits for them, and re-layouts  4.98 us
    dot_general x1, matrix products, token_space_whiten(): jnp.einsum('tc,uc->tu', sides, sides, preferred_element_type=jnp.float32)  4.53 us
    dot_general x1, matrix products, planes(): jnp.einsum('ta,btc->abc', acts_low, grads_low, preferred_element_type=jnp...  3.19 us
    convert_element_type x1, other arithmetic, token_space_whiten(): low = (gram / scale).astype(jnp.bfloat16)  2.78 us

profile of v2, /device:TPU:0, one launch (start us, length us, event | category | flops | bytes accessed | tf_op | source)
XLA Modules:
  0.0 110.3 jit_solution(13446917249012200425)
XLA Ops:
  0.6 1.5 %fusion.26 = (bf16[128,1,512]{2,1,0:T(2,128)(2,1)S(1)}, bf16[128,1,512]{2,1,0:T(2,128)(2,1)S(1)}) fusion(bf16[128,2,512]{2,1,0:T(2,128)(2,1)} %param.3), kind=kLoop, calls=%fused_computation.49 | loop fusion | bytes 524288 | tf_op jit(solution)/shard_map/slice | solution.py:450
  2.2 1.5 %fusion.27 = (bf16[128,1,512]{2,1,0:T(2,128)(2,1)S(1)}, bf16[128,1,512]{2,1,0:T(2,128)(2,1)S(1)}) fusion(bf16[128,2,512]{2,1,0:T(2,128)(2,1)} %param.4), kind=kLoop, calls=%fused_computation.50 | loop fusion | bytes 524288 | tf_op jit(solution)/shard_map/slice | solution.py:450
  3.8 0.9 pad_maximum_fusion.pieces
  4.6 34.7 %collect.1 = (bf16[1024,2048]{1,0:T(8,128)(2,1)}, bf16[2,128,2048]{2,1,0:T(8,128)(2,1)}) custom-call(bf16[4,128,512]{2,1,0:T(8,128)(2,1)} %pad_maximum_fusion.pieces), custom_call_target="tpu_custom_call" | custom-call | tf_op jit(solution)/shard_map/collect/pallas_call | solution.py:217
  39.3 0.0 copy-start.1
  39.3 6.7 %fusion.14 = bf16[128,2,512]{2,0,1:T(8,128)(2,1)S(1)} fusion(bf16[2,64,2,8,2048]{4,3,2,1,0:T(8,128)(2,1)} %bitcast.34, bf16[2,128,2048]{2,1,0:T(8,128)(2,1)} %get-tuple-element.9), kind=kOutput, calls=%fused_computation.23 | convolution fusion | flops 1073872896 | bytes 9699328 | tf_op jit(solution)/shard_map/jtq,bcjq->tbc/dot_general | solution.py:458
  46.1 1.0 copy.12
  47.0 0.0 copy-done.1
  47.0 0.6 convert_reduce_fusion
  47.7 4.5 %multiply_reduce_fusion.1 = (f32[1024]{0:T(1024)S(1)}, f32[1024,1024]{0,1:T(8,128)S(1)}) fusion(f32[1024]{0:T(1024)S(1)} %broadcast_multiply_fusion.1, bf16[1024,2048]{1,0:T(8,128)(2,1)S(1)} %copy-done.1), kind=kOutput, calls=%fused_computation.6 | convolution fusion | flops 4297063424 | bytes 8396800 | tf_op jit(solution)/shard_map/tc,uc->tu/dot_general | solution.py:409
  52.2 0.0 copy-start
  52.2 1.9 %copy-done = f32[1024,1024]{0,1:T(8,128)} copy-done((f32[1024,1024]{0,1:T(8,128)}, f32[1024,1024]{0,1:T(8,128)S(1)}, u32[]{:S(2)}) %copy-start) | copy-done | bytes 4194328
  54.2 0.3 multiply_reduce_fusion
  54.5 0.6 multiply_reduce_fusion.2
  60.7 2.8 %divide_convert_fusion = bf16[1024,1024]{0,1:T(8,128)(2,1)S(1)} fusion(f32[1024,1024]{0,1:T(8,128)} %copy-done, f32[]{:T(128)S(6)} %div.80), kind=kLoop, calls=%fused_computation.4 | loop fusion | flops 3145728 | bytes 6291460 | tf_op jit(solution)/shard_map/convert_element_type | solution.py:428
  63.5 2.1 %fusion.8 = f32[1024,256]{1,0:T(8,128)S(1)} fusion(bf16[1024,1024]{0,1:T(8,128)(2,1)S(1)} %divide_convert_fusion, f32[]{:T(128)S(6)} %div.83, bf16[1024,2048]{1,0:T(8,128)(2,1)} %get-tuple-element.6, s32[]{:T(128)S(6)} %select_n.3), kind=kOutput, calls=%fused_computation.17 | convolution fusion | flops 538181632 | bytes 4195840 | tf_op jit(solution)/shard_map/tu,uc->tc/dot_general | solution.py:432
  65.7 0.8 convolution_add_fusion.2
  66.4 0.7 fusion.7
  67.2 1.8 %fusion.10.low = bf16[1024,256]{1,0:T(8,128)(2,1)} fusion(bf16[1024,1024]{0,1:T(8,128)(2,1)S(1)} %divide_convert_fusion, f32[1024,256]{1,0:T(8,128)S(1)} %fusion.7, f32[1024,256]{1,0:T(8,128)S(1)} %fusion.8, f32[]{:T(128)S(6)} %sqrt.3, f32[]{:T(128)S(6)} %mul.116), kind=kOutput, calls=%fused_computation.21 | convolution fusion | flops 540016640 | bytes 4718600 | tf_op jit(solution)/shard_map/tu,uc->tc/dot_general | solution.py:432
  69.0 36.0 %deliver.1 = (bf16[2,1024,512]{2,1,0:T(8,128)(2,1)}, bf16[1024,512]{1,0:T(8,128)(2,1)}) custom-call(bf16[1024,256]{1,0:T(8,128)(2,1)} %fusion.10.low), custom_call_target="tpu_custom_call" | custom-call | tf_op jit(solution)/shard_map/deliver/pallas_call | solution.py:383
  105.0 3.2 %multiply_convert_fusion = bf16[512,2,512]{2,0,1:T(8,128)(2,1)S(1)} fusion(bf16[2,1024,512]{2,1,0:T(8,128)(2,1)} %get-tuple-element.8, bf16[1024,512]{1,0:T(8,128)(2,1)} %get-tuple-element.7), kind=kOutput, calls=%fused_computation.7 | convolution fusion | flops 1074790400 | bytes 4194304 | tf_op jit(solution)/shard_map/ta,btc->abc/dot_general | solution.py:455
  108.2 2.0 %copy.11 = bf16[512,2,512]{2,1,0:T(2,128)(2,1)} copy(bf16[512,2,512]{2,0,1:T(8,128)(2,1)S(1)} %multiply_convert_fusion) | data formatting | bytes 2097152
  (4 shorter events, 0.1 us)
Async XLA Ops:
  39.3 7.7 %copy-start.1 = (bf16[1024,2048]{1,0:T(8,128)(2,1)S(1)}, bf16[1024,2048]{1,0:T(8,128)(2,1)}, u32[]{:S(2)}) copy-start(bf16[1024,2048]{1,0:T(8,128)(2,1)} %get-tuple-element.6) | copy-start | bytes 12582916
  52.2 2.0 %copy-start = (f32[1024,1024]{0,1:T(8,128)}, f32[1024,1024]{0,1:T(8,128)S(1)}, u32[]{:S(2)}) copy-start(f32[1024,1024]{0,1:T(8,128)S(1)} %get-tuple-element.24) | copy-start | bytes 12582916

commit v3 on v2

--- a/solution.py
+++ b/solution.py
@@ -131,6 +131,10 @@
     )
 
 
+def held(z):
+    return z + (z + 2) // 3 - 3 * (z // 3)
+
+
 def neighbours():
     z, o, y = lax.axis_index("tok"), lax.axis_index("out"), lax.axis_index("grp")
     ox = lax.rem(o + 2, 4)
@@ -141,7 +145,7 @@
     return z, o, y, ox, oc, zs, peers, at(z, o, 1 - y), at(z, ox, y), at(z, oc, y)
 
 
-def collect_kernel(pieces, sides, grads, send, recv, grads_recv, local):
+def collect_kernel(pieces, sides, send, recv, local):
     z, o, y, ox, oc, zs, z_peers, y_peer, x_peer, c_peer = neighbours()
     rows, width = pieces.shape[1:]
     count = [0]
@@ -152,9 +156,6 @@
             pl.ds(pl.multiple_of(oi * width, width), width),
         ]
 
-    def band(oi):
-        return grads.at[:, :, pl.ds(pl.multiple_of(oi * width, width), width)]
-
     sent = []
 
     def push(src, dst, sem, peer):
@@ -177,15 +178,10 @@
 
     greet(z_peers + [y_peer, x_peer, c_peer])
     for j in (1, 3, 2):
-        push(pieces.at[zs[j]], tile(o, y, z), sem_of(o, y, z), z_peers[j - 1])
-    own = pltpu.make_async_copy(pieces.at[z], tile(o, y, z), local.at[0])
+        push(pieces.at[held(zs[j])], tile(o, y, z), sem_of(o, y, z), z_peers[j - 1])
+    own = pltpu.make_async_copy(pieces.at[held(z)], tile(o, y, z), local)
     own.start()
-    forward(pieces.at[z], o, y, z, (y_peer, x_peer, c_peer))
-    low = pieces.at[1:3]
-    own_grads = pltpu.make_async_copy(low, band(o), local.at[1])
-    own_grads.start()
-    for peer in (x_peer, c_peer):
-        push(low, band(o), grads_recv.at[o], peer)
+    forward(pieces.at[held(z)], o, y, z, (y_peer, x_peer, c_peer))
     for j in (1, 3, 2):
         forward(arrived(o, y, zs[j]), o, y, zs[j], (y_peer, x_peer, c_peer))
     for step, j in enumerate(HOPS):
@@ -193,9 +189,6 @@
         forward(ref, o, 1 - y, zs[j], (x_peer, c_peer) if step % 2 == 0 else (c_peer,))
         ref = arrived(ox, y, zs[j])
         forward(ref, ox, y, zs[j], (y_peer, c_peer) if step % 2 == 1 else (c_peer,))
-    ref = band(ox)
-    remote(ref, ref, send.at[0], grads_recv.at[ox], c_peer).wait_recv()
-    push(ref, ref, grads_recv.at[ox], c_peer)
     for j in HOPS:
         forward(arrived(ox, 1 - y, zs[j]), ox, 1 - y, zs[j], (c_peer,))
     oxc = lax.rem(oc + 2, 4)
@@ -203,37 +196,30 @@
         for yi in (y, 1 - y):
             for j in HOPS:
                 arrived(oi, yi, zs[j])
-        ref = band(oi)
-        remote(ref, ref, send.at[0], grads_recv.at[oi], c_peer).wait_recv()
     own.wait()
-    own_grads.wait()
     for copy in sent:
         copy.wait_send()
 
 
 def collect(pieces):
-    count, rows, width = pieces.shape
-    sends = 3 + 3 * 4 + 3 * 4 + 4 + 3 + 4
+    _, rows, width = pieces.shape
+    sends = 3 + 3 * 4 + 3 * 4 + 4
     return pl.pallas_call(
         collect_kernel,
-        out_shape=(
-            jax.ShapeDtypeStruct((rows * 8, width * 4), pieces.dtype),
-            jax.ShapeDtypeStruct((count // 2, rows, width * 4), pieces.dtype),
-        ),
+        out_shape=jax.ShapeDtypeStruct((rows * 8, width * 4), pieces.dtype),
         in_specs=[pl.BlockSpec(memory_space=pltpu.VMEM)],
-        out_specs=(pl.BlockSpec(memory_space=pltpu.VMEM), pl.BlockSpec(memory_space=pltpu.VMEM)),
+        out_specs=pl.BlockSpec(memory_space=pltpu.VMEM),
         scratch_shapes=[
             pltpu.SemaphoreType.DMA((sends,)),
             pltpu.SemaphoreType.DMA((32,)),
-            pltpu.SemaphoreType.DMA((4,)),
-            pltpu.SemaphoreType.DMA((2,)),
+            pltpu.SemaphoreType.DMA,
         ],
         compiler_params=pltpu.CompilerParams(collective_id=0, has_side_effects=True),
         name="collect",
     )(pieces)
 
 
-def deliver_kernel(low, grads, acts, g_send, y_send, g_recv, y_recv, a_send, a_recv, hub_send, hub_recv, local):
+def deliver_kernel(low, pieces, grads, acts, raw, r_send, r_recv, g_send, y_send, g_recv, y_recv, a_send, a_recv, hub_send, hub_recv, local):
     z, o, y, ox, oc, zs, z_peers, y_peer, x_peer, c_peer = neighbours()
     tokens, part = low.shape
     rows = tokens // CHUNKS
@@ -251,6 +237,19 @@
         {"tok": zs[j], "out": o, "grp": 1 - y} for j in (1, 2, 3)
     ]
     greet(greet_all)
+    width = pieces.shape[2]
+
+    def band(oi):
+        return raw.at[:, :, pl.ds(pl.multiple_of(oi * width, width), width)]
+
+    own_raw = pieces.at[2:4]
+    raw_local = pltpu.make_async_copy(own_raw, band(o), r_send.at[3])
+    raw_x = remote(own_raw, band(o), r_send.at[0], r_recv.at[0], x_peer)
+    raw_c = remote(own_raw, band(o), r_send.at[1], r_recv.at[1], c_peer)
+    raw_xc = remote(band(ox), band(ox), r_send.at[2], r_recv.at[2], c_peer)
+    raw_x.start()
+    raw_c.start()
+    raw_local.start()
 
     def span(c):
         return pl.ds(c * rows, rows)
@@ -348,8 +347,15 @@
                 y_copy(ref, b, c).start()
 
         hub_step(c)
+    raw_x.wait_recv()
+    raw_xc.start()
     for c in range(CHUNKS):
         relay_step(c)
+    raw_c.wait_recv()
+    raw_xc.wait()
+    raw_x.wait_send()
+    raw_c.wait_send()
+    raw_local.wait()
     for c in range(CHUNKS):
         for b in range(2):
             ref = g_tile(b, 1 - y, c)
@@ -377,18 +383,23 @@
                 from_hub(yi, c, 1, c_peer).wait_send()
 
 
-def deliver(low):
+def deliver(low, pieces):
     tokens, part = low.shape
+    _, rows, width = pieces.shape
     dma = pltpu.SemaphoreType.DMA
+    vmem = pl.BlockSpec(memory_space=pltpu.VMEM)
     return pl.pallas_call(
         deliver_kernel,
         out_shape=(
             jax.ShapeDtypeStruct((2, tokens, 2 * part), low.dtype),
             jax.ShapeDtypeStruct((tokens, 2 * part), low.dtype),
+            jax.ShapeDtypeStruct((2, rows, 4 * width), low.dtype),
         ),
-        in_specs=[pl.BlockSpec(memory_space=pltpu.VMEM)],
-        out_specs=(pl.BlockSpec(memory_space=pltpu.VMEM), pl.BlockSpec(memory_space=pltpu.VMEM)),
+        in_specs=[vmem, vmem],
+        out_specs=(vmem, vmem, vmem),
         scratch_shapes=[
+            dma((4,)),
+            dma((3,)),
             dma((3 * CHUNKS,)),
             dma((2 * CHUNKS,)),
             dma((2 * CHUNKS,)),
@@ -401,45 +412,110 @@
         ],
         compiler_params=pltpu.CompilerParams(collective_id=1, has_side_effects=True),
         name="deliver",
-    )(low)
-
-
-def token_space_whiten(sides, cols):
+    )(low, pieces)
+
+
+def whiten_kernel(sides, out, gram, low, ray, head, tail, left, right):
     tokens, block = sides.shape
-    gram = jnp.einsum("tc,uc->tu", sides, sides, preferred_element_type=jnp.float32) / tokens
-    ray_0 = jnp.sum(sides.astype(jnp.float32), axis=1)
-    ray_1 = jnp.sum(gram * ray_0[None, :], axis=1) + DAMPING * ray_0
-    ray_2 = jnp.sum(gram * ray_1[None, :], axis=1) + DAMPING * ray_1
+    part = out.shape[1]
+    tile = min(256, tokens)
+    steps = tokens // tile
+    across = (((1,), (1,)), ((), ()))
+    ones = jnp.ones((8, block), sides.dtype)
+    ray_0 = lax.dot_general(ones, sides[...], across, preferred_element_type=jnp.float32)[0:1]
+
+    def span(i):
+        return pl.ds(pl.multiple_of(i * tile, tile), tile)
+
+    def gram_step(i, ray_2):
+        product = lax.dot_general(
+            sides[span(i), :], sides[...], across, preferred_element_type=jnp.float32
+        )
+        row_ids = i * tile + lax.broadcasted_iota(jnp.int32, (tile, tokens), 0)
+        col_ids = lax.broadcasted_iota(jnp.int32, (tile, tokens), 1)
+        product = product / tokens + jnp.where(row_ids == col_ids, DAMPING, 0.0)
+        gram[span(i), :] = product
+        column = jnp.sum(product * ray_0, axis=1, keepdims=True)
+        ray[:, span(i)] = jnp.transpose(jnp.broadcast_to(column, (tile, 128)))[0:8]
+        return ray_2 + jnp.sum(product * column, axis=0, keepdims=True)
+
+    ray_2 = lax.fori_loop(0, steps, gram_step, jnp.zeros((1, tokens), jnp.float32))
+    ray_1 = ray[0:1, :]
+
+    def pair(a, b):
+        return jnp.sum(a * b, axis=1, keepdims=True)
+
     dots = [
-        jnp.sum(ray_0 * ray_0),
-        jnp.sum(ray_0 * ray_1),
-        jnp.sum(ray_1 * ray_1),
-        jnp.sum(ray_1 * ray_2),
-        jnp.sum(ray_2 * ray_2),
+        pair(ray_0, ray_0),
+        pair(ray_0, ray_1),
+        pair(ray_1, ray_1),
+        pair(ray_1, ray_2),
+        pair(ray_2, ray_2),
     ]
 
     def moment(power):
-        total = DAMPING**power * block
+        total = jnp.full((1, 1), DAMPING**power * block, jnp.float32)
         for i in range(power):
             total = total + DAMPING ** (power - 1 - i) * dots[i] / tokens
         return total
 
     scale = moment(2 * POWER - 1) / moment(2 * POWER - 2)
-    low = (gram / scale).astype(jnp.bfloat16)
-    shift = DAMPING / scale
-
-    def apply(value):
-        product = jnp.einsum(
-            "tu,uc->tc", low, value.astype(jnp.bfloat16), preferred_element_type=jnp.float32
-        )
-        return product + shift * value
-
-    def first(value):
-        return (3.0 * value - apply(value)) / 2.0
-
-    head = first(cols.astype(jnp.float32))
-    tail = first(first(apply(head)))
-    return ((3.0 * head - tail) / 2.0 / jnp.sqrt(scale)).astype(jnp.bfloat16)
+    inverse = 1.0 / scale
+    root = 1.0 / jnp.sqrt(scale)
+    start = lax.axis_index("out") * (2 * part) + lax.axis_index("grp") * part
+    cols = pl.ds(pl.multiple_of(start, part), part)
+
+    @pl.loop(0, steps)
+    def _(i):
+        low[span(i), :] = (gram[span(i), :] * inverse).astype(low.dtype)
+        left[span(i), :] = sides[span(i), cols]
+
+    def apply(i, source):
+        return jnp.dot(low[span(i), :], source[...], preferred_element_type=jnp.float32)
+
+    @pl.loop(0, steps)
+    def _(i):
+        value = sides[span(i), cols].astype(jnp.float32)
+        value = 1.5 * value - 0.5 * apply(i, left)
+        head[span(i), :] = value
+        right[span(i), :] = value.astype(right.dtype)
+
+    @pl.loop(0, steps)
+    def _(i):
+        value = apply(i, right)
+        tail[span(i), :] = value
+        left[span(i), :] = value.astype(left.dtype)
+
+    @pl.loop(0, steps)
+    def _(i):
+        value = 1.5 * tail[span(i), :] - 0.5 * apply(i, left)
+        tail[span(i), :] = value
+        right[span(i), :] = value.astype(right.dtype)
+
+    @pl.loop(0, steps)
+    def _(i):
+        value = 1.5 * tail[span(i), :] - 0.5 * apply(i, right)
+        out[span(i), :] = ((1.5 * head[span(i), :] - 0.5 * value) * root).astype(out.dtype)
+
+
+def whiten(sides, part):
+    tokens, block = sides.shape
+    return pl.pallas_call(
+        whiten_kernel,
+        out_shape=jax.ShapeDtypeStruct((tokens, part), sides.dtype),
+        in_specs=[pl.BlockSpec(memory_space=pltpu.VMEM)],
+        out_specs=pl.BlockSpec(memory_space=pltpu.VMEM),
+        scratch_shapes=[
+            pltpu.VMEM((tokens, tokens), jnp.float32),
+            pltpu.VMEM((tokens, tokens), sides.dtype),
+            pltpu.VMEM((8, tokens), jnp.float32),
+            pltpu.VMEM((tokens, part), jnp.float32),
+            pltpu.VMEM((tokens, part), jnp.float32),
+            pltpu.VMEM((tokens, part), sides.dtype),
+            pltpu.VMEM((tokens, part), sides.dtype),
+        ],
+        name="whiten",
+    )(sides)
 
 
 def planes(activations, out_grads, weight):
@@ -447,11 +523,8 @@
     block = width * lax.axis_size("out")
     part = width // lax.axis_size("grp")
     token_count = tok_dev * lax.axis_size(("tok", "grp"))
-    pieces = jnp.stack([activations[:, 0], out_grads[:, 0], out_grads[:, 1], activations[:, 1]])
-    sides, grads_whole = collect(pieces)
-    start = lax.axis_index("out") * width + lax.axis_index("grp") * part
-    cols = lax.dynamic_slice_in_dim(sides, start, part, 1)
-    grads_low, acts_low = deliver(token_space_whiten(sides, cols))
+    pieces = jnp.swapaxes(jnp.concatenate([activations, out_grads], axis=1), 0, 1)
+    grads_low, acts_low, grads_whole = deliver(whiten(collect(pieces), part), pieces)
     update = jnp.einsum("ta,btc->abc", acts_low, grads_low, preferred_element_type=jnp.float32)
     update = (update / math.sqrt(token_count)).astype(jnp.bfloat16)
     weight_rows = weight.reshape(blocks, width, blocks, block)

time: 111 us -> 102 us (0.919)
  Pallas kernels: 70.7 us -> 85.4 us
  matrix products: 19.9 us -> 9.52 us
  between operations: 6.33 us -> 0.67 us
  other arithmetic: 5.24 us -> 0.84 us
  local copies, waits for them, and re-layouts: 8.08 us -> 4.99 us
    pallas_call x1 -> x2, Pallas kernels: 34.7 us -> 47.3 us  [the longest x1 32.1 us: collect(): pl.pallas_call(collect_kernel, out_shape=jax.ShapeDtypeStruct((rows * 8,...]
    dot_general x5 -> x0, matrix products: 10 us -> none  [the longest x4 5.48 us: apply(): jnp.einsum('tu,uc->tc', low, value.astype(jnp.bfloat16), preferred_elemen...]
    slice x2 -> x0, local copies, waits for them, and re-layouts: 3.03 us -> none  [the longest x1 1.53 us: planes(): out_grads[:, 0]]
    convert_element_type x1 -> x0, other arithmetic: 2.78 us -> none  [token_space_whiten(): low = (gram / scale).astype(jnp.bfloat16)]
    pallas_call x1, Pallas kernels: 36 us -> 38.1 us  [deliver(): pl.pallas_call(deliver_kernel, out_shape=(jax.ShapeDtypeStruct((2, tokens...]
    reduce_sum x3 -> x0, other arithmetic: 1.59 us -> none  [the longest x1 0.63 us: token_space_whiten(): jnp.sum(ray_2 * ray_2)]
where the time goes in v3:
time: 102 us; the launch traced here: 101 us
  Pallas kernels  85.4 us (84%)
  matrix products  9.52 us (9%)
  local copies, waits for them, and re-layouts  4.99 us (5%)
    pallas_call x1, Pallas kernels, deliver(): pl.pallas_call(deliver_kernel, out_shape=(jax.ShapeDtypeStruct((2, tokens...  38.1 us
    pallas_call x1, Pallas kernels, collect(): pl.pallas_call(collect_kernel, out_shape=jax.ShapeDtypeStruct((rows * 8,...  32.1 us
    pallas_call x1, Pallas kernels, whiten(): pl.pallas_call(whiten_kernel, out_shape=jax.ShapeDtypeStruct((tokens, par...  15.2 us
    dot_general x1, matrix products, planes(): jnp.einsum('jtq,bcjq->tbc', grads_whole, weight_rows, preferred_element_t...  6.33 us
    unnamed x6, local copies, waits for them, and re-layouts  4.99 us
    dot_general x1, matrix products, planes(): jnp.einsum('ta,btc->abc', acts_low, grads_low, preferred_element_type=jnp...  3.19 us

profile of v3, /device:TPU:0, one launch (start us, length us, event | category | flops | bytes accessed | tf_op | source)
XLA Modules:
  0.0 101.4 jit_solution(15633424852062390016)
XLA Ops:
  0.6 1.0 copy.5
  1.6 1.0 copy.6
  2.6 0.8 maximum_bitcast_fusion.pieces
  3.4 32.1 %collect.1.sides = bf16[1024,2048]{1,0:T(8,128)(2,1)} custom-call(bf16[4,128,512]{2,1,0:T(8,128)(2,1)} %maximum_bitcast_fusion.pieces), custom_call_target="tpu_custom_call" | custom-call | tf_op jit(solution)/shard_map/collect/pallas_call | solution.py:207
  35.5 15.2 %whiten.1.low = bf16[1024,256]{1,0:T(8,128)(2,1)} custom-call(bf16[1024,2048]{1,0:T(8,128)(2,1)} %collect.1.sides), custom_call_target="tpu_custom_call" | custom-call | tf_op jit(solution)/shard_map/whiten/pallas_call | solution.py:503
  50.8 38.1 %deliver.1 = (bf16[2,1024,512]{2,1,0:T(8,128)(2,1)}, bf16[1024,512]{1,0:T(8,128)(2,1)}, bf16[2,128,2048]{2,1,0:T(8,128)(2,1)}) custom-call(bf16[1024,256]{1,0:T(8,128)(2,1)} %whiten.1.low, bf16[4,128,512]{2,1,0:T(8,128)(2,1)} %maximum_bitcast_fusion.pieces), custom_call_target="tpu_custom_call" | custom-call | tf_op jit(solution)/shard_map/deliver/pallas_call | solution.py:391
  88.9 3.2 %multiply_convert_fusion = bf16[512,2,512]{2,0,1:T(8,128)(2,1)S(1)} fusion(bf16[2,1024,512]{2,1,0:T(8,128)(2,1)} %get-tuple-element.6, bf16[1024,512]{1,0:T(8,128)(2,1)} %get-tuple-element.5), kind=kOutput, calls=%fused_computation.3 | convolution fusion | flops 1074790400 | bytes 4194304 | tf_op jit(solution)/shard_map/ta,btc->abc/dot_general | solution.py:528
  92.1 0.0 copy-start
  92.1 2.0 %copy.9 = bf16[512,2,512]{2,1,0:T(2,128)(2,1)} copy(bf16[512,2,512]{2,0,1:T(8,128)(2,1)S(1)} %multiply_convert_fusion) | data formatting | bytes 2097152
  94.1 0.0 copy-done
  94.1 6.3 %fusion.6 = bf16[128,2,512]{2,0,1:T(8,128)(2,1)S(1)} fusion(bf16[2,64,2,8,2048]{4,3,2,1,0:T(8,128)(2,1)} %bitcast.22, bf16[2,128,2048]{2,1,0:T(8,128)(2,1)S(1)} %copy-done), kind=kOutput, calls=%fused_computation.5 | convolution fusion | flops 1073872896 | bytes 9699328 | tf_op jit(solution)/shard_map/jtq,bcjq->tbc/dot_general | solution.py:531
  100.5 1.0 copy.10
Async XLA Ops:
  92.1 2.1 %copy-start = (bf16[2,128,2048]{2,1,0:T(8,128)(2,1)S(1)}, bf16[2,128,2048]{2,1,0:T(8,128)(2,1)}, u32[]{:S(2)}) copy-start(bf16[2,128,2048]{2,1,0:T(8,128)(2,1)} %get-tuple-element.7) | copy-start | bytes 3145732

commit v4 on v3

--- a/solution.py
+++ b/solution.py
@@ -115,7 +115,8 @@
 
 MESH = pl.DeviceIdType.MESH
 HOPS = (0, 1, 3, 2)
-CHUNKS = 4
+CHUNKS = 8
+SPLIT = 2
 
 
 def greet(peers):
@@ -147,63 +148,70 @@
 
 def collect_kernel(pieces, sides, send, recv, local):
     z, o, y, ox, oc, zs, z_peers, y_peer, x_peer, c_peer = neighbours()
-    rows, width = pieces.shape[1:]
-    count = [0]
-
-    def tile(oi, yi, zi):
+    width = pieces.shape[2]
+    rows = pieces.shape[1] // SPLIT
+    sent = []
+
+    def tile(oi, yi, zi, s):
         return sides.at[
-            pl.ds(pl.multiple_of((yi * 4 + zi) * rows, rows), rows),
+            pl.ds(pl.multiple_of(((yi * 4 + zi) * SPLIT + s) * rows, rows), rows),
             pl.ds(pl.multiple_of(oi * width, width), width),
         ]
 
-    sent = []
-
-    def push(src, dst, sem, peer):
-        copy = remote(src, dst, send.at[count[0]], sem, peer)
-        count[0] += 1
+    def piece(zi, s):
+        return pieces.at[held(zi), pl.ds(s * rows, rows), :]
+
+    def push(src, where, peer):
+        copy = remote(src, tile(*where), send.at[len(sent)], sem_of(*where), peer)
         copy.start()
         sent.append(copy)
 
-    def sem_of(oi, yi, zi):
-        return recv.at[oi * 8 + yi * 4 + zi]
-
-    def arrived(oi, yi, zi):
-        ref = tile(oi, yi, zi)
-        remote(ref, ref, send.at[0], sem_of(oi, yi, zi), c_peer).wait_recv()
+    def sem_of(oi, yi, zi, s):
+        return recv.at[(oi * 8 + yi * 4 + zi) * SPLIT + s]
+
+    def arrived(*where):
+        ref = tile(*where)
+        remote(ref, ref, send.at[0], sem_of(*where), c_peer).wait_recv()
         return ref
 
-    def forward(src, oi, yi, zi, peers):
+    def forward(src, where, peers):
         for peer in peers:
-            push(src, tile(oi, yi, zi), sem_of(oi, yi, zi), peer)
+            push(src, where, peer)
 
     greet(z_peers + [y_peer, x_peer, c_peer])
-    for j in (1, 3, 2):
-        push(pieces.at[held(zs[j])], tile(o, y, z), sem_of(o, y, z), z_peers[j - 1])
-    own = pltpu.make_async_copy(pieces.at[held(z)], tile(o, y, z), local)
-    own.start()
-    forward(pieces.at[held(z)], o, y, z, (y_peer, x_peer, c_peer))
-    for j in (1, 3, 2):
-        forward(arrived(o, y, zs[j]), o, y, zs[j], (y_peer, x_peer, c_peer))
-    for step, j in enumerate(HOPS):
-        ref = arrived(o, 1 - y, zs[j])
-        forward(ref, o, 1 - y, zs[j], (x_peer, c_peer) if step % 2 == 0 else (c_peer,))
-        ref = arrived(ox, y, zs[j])
-        forward(ref, ox, y, zs[j], (y_peer, c_peer) if step % 2 == 1 else (c_peer,))
-    for j in HOPS:
-        forward(arrived(ox, 1 - y, zs[j]), ox, 1 - y, zs[j], (c_peer,))
+    order = [(j, s) for j in HOPS for s in range(SPLIT)]
+    owns = []
+    for s in range(SPLIT):
+        for j in (1, 3, 2):
+            push(piece(zs[j], s), (o, y, z, s), z_peers[j - 1])
+        forward(piece(z, s), (o, y, z, s), (y_peer, x_peer, c_peer))
+        owns.append(pltpu.make_async_copy(piece(z, s), tile(o, y, z, s), local.at[s]))
+        owns[-1].start()
+    for j, s in order[SPLIT:]:
+        where = (o, y, zs[j], s)
+        forward(arrived(*where), where, (y_peer, x_peer, c_peer))
+    for j, s in order:
+        where = (o, 1 - y, zs[j], s)
+        forward(arrived(*where), where, (x_peer, c_peer) if s % 2 == 0 else (c_peer,))
+        where = (ox, y, zs[j], s)
+        forward(arrived(*where), where, (y_peer, c_peer) if s % 2 == 1 else (c_peer,))
+    for j, s in order:
+        where = (ox, 1 - y, zs[j], s)
+        forward(arrived(*where), where, (c_peer,))
     oxc = lax.rem(oc + 2, 4)
     for oi in (oc, oxc):
         for yi in (y, 1 - y):
-            for j in HOPS:
-                arrived(oi, yi, zs[j])
-    own.wait()
+            for j, s in order:
+                arrived(oi, yi, zs[j], s)
+    for copy in owns:
+        copy.wait()
     for copy in sent:
         copy.wait_send()
 
 
 def collect(pieces):
     _, rows, width = pieces.shape
-    sends = 3 + 3 * 4 + 3 * 4 + 4
+    sends = (3 + 3 * 4 + 3 * 4 + 4) * SPLIT
     return pl.pallas_call(
         collect_kernel,
         out_shape=jax.ShapeDtypeStruct((rows * 8, width * 4), pieces.dtype),
@@ -211,33 +219,36 @@
         out_specs=pl.BlockSpec(memory_space=pltpu.VMEM),
         scratch_shapes=[
             pltpu.SemaphoreType.DMA((sends,)),
-            pltpu.SemaphoreType.DMA((32,)),
-            pltpu.SemaphoreType.DMA,
+            pltpu.SemaphoreType.DMA((32 * SPLIT,)),
+            pltpu.SemaphoreType.DMA((SPLIT,)),
         ],
         compiler_params=pltpu.CompilerParams(collective_id=0, has_side_effects=True),
         name="collect",
     )(pieces)
 
 
-def deliver_kernel(low, pieces, grads, acts, raw, r_send, r_recv, g_send, y_send, g_recv, y_recv, a_send, a_recv, hub_send, hub_recv, local):
+def deliver_kernel(
+    low, pieces, weight, grads, acts, product,
+    raw, held_weight, w_sem, r_send, r_recv, g_send, y_send, g_recv, y_recv,
+    a_send, a_recv, x_send, c_send, c_recv, local,
+):
     z, o, y, ox, oc, zs, z_peers, y_peer, x_peer, c_peer = neighbours()
     tokens, part = low.shape
     rows = tokens // CHUNKS
-    oxc = lax.rem(oc + 2, 4)
-    row = 2 * z + y
-    hub = lax.rem(row, 4)
+    width = pieces.shape[2]
+    block = raw.shape[2]
+    strip = width // 2
     is_grad = (z == 1) | (z == 2)
+    is_act = jnp.logical_not(is_grad)
     mine = z - 1
-    base = (z // 3) * 2
-    goal_z, goal_y = base + o // 2, lax.rem(o, 2)
-    stays = (goal_z == z) & (goal_y == y)
-    goal = {"tok": goal_z, "out": o, "grp": goal_y}
-    source_z = (row // 4) * 3
-    greet_all = z_peers + [y_peer, x_peer, c_peer] + [
-        {"tok": zs[j], "out": o, "grp": 1 - y} for j in (1, 2, 3)
-    ]
-    greet(greet_all)
-    width = pieces.shape[2]
+    h = lax.rem(o, 2)
+    goal_z = (z // 3) * 2 + o // 2
+    stays = goal_z == z
+    goal = {"tok": goal_z, "out": o, "grp": y}
+    is_hub = o // 2 == lax.rem(z, 2)
+    not_hub = jnp.logical_not(is_hub)
+    here = is_act & stays
+    greet(z_peers + [y_peer, x_peer, c_peer])
 
     def band(oi):
         return raw.at[:, :, pl.ds(pl.multiple_of(oi * width, width), width)]
@@ -257,20 +268,20 @@
     def piece(c):
         return low.at[span(c), :]
 
-    def half(yi):
-        return pl.ds(pl.multiple_of(yi * part, part), part)
+    def half(i):
+        return pl.ds(pl.multiple_of(i * part, part), part)
 
     def g_tile(b, yi, c):
         return grads.at[b, span(c), half(yi)]
 
-    def a_tile(yi, c):
-        return acts.at[span(c), half(yi)]
+    def a_tile(i, c):
+        return acts.at[span(c), half(i)]
 
     def own_grad(c):
         return pltpu.make_async_copy(piece(c), g_tile(mine, y, c), local.at[c])
 
     def own_act(c):
-        return pltpu.make_async_copy(piece(c), a_tile(y, c), local.at[c])
+        return pltpu.make_async_copy(piece(c), a_tile(h, c), local.at[c])
 
     def to_plane(c, j):
         return remote(
@@ -278,18 +289,16 @@
         )
 
     def y_copy(src, b, c):
-        return remote(
-            src, g_tile(b, y, c), y_send.at[b * CHUNKS + c], y_recv.at[b * CHUNKS + c], y_peer
-        )
+        return remote(src, g_tile(b, y, c), y_send.at[b * CHUNKS + c], y_recv.at[b * CHUNKS + c], y_peer)
 
     def to_hub(c):
-        return remote(piece(c), a_tile(y, c), a_send.at[c], a_recv.at[y * CHUNKS + c], goal)
-
-    def from_hub(yi, c, way, peer):
-        ref = a_tile(yi, c)
-        return remote(
-            ref, ref, hub_send.at[way * 2 * CHUNKS + yi * CHUNKS + c], hub_recv.at[yi * CHUNKS + c], peer
-        )
+        return remote(piece(c), a_tile(h, c), a_send.at[c], a_recv.at[c], goal)
+
+    def over_x(c):
+        return remote(a_tile(h, c), a_tile(h, c), x_send.at[c], a_recv.at[c], x_peer)
+
+    def over_core(c):
+        return remote(a_tile(h, c), a_tile(h, c), c_send.at[c], c_recv.at[c], c_peer)
 
     for c in range(CHUNKS):
 
@@ -300,42 +309,53 @@
             y_copy(piece(c), mine, c).start()
             own_grad(c).start()
 
-        @pl.when(jnp.logical_not(is_grad) & stays)
+        @pl.when(here)
         def _():
             own_act(c).start()
 
-        @pl.when(jnp.logical_not(is_grad) & jnp.logical_not(stays))
+        @pl.when(is_act & jnp.logical_not(stays))
         def _():
             to_hub(c).start()
 
-    def hub_step(c):
-        for yi in range(2):
-            here = (source_z == z) & (y == yi)
-
-            @pl.when((o == hub) & here)
-            def _():
-                own_act(c).wait()
-
-            @pl.when((o == hub) & jnp.logical_not(here))
-            def _():
-                ref = a_tile(yi, c)
-                remote(ref, ref, a_send.at[0], a_recv.at[yi * CHUNKS + c], c_peer).wait_recv()
-
-            @pl.when(o == hub)
-            def _():
-                from_hub(yi, c, 0, x_peer).start()
-                from_hub(yi, c, 1, c_peer).start()
-
-    def relay_step(c):
-        for yi in range(2):
-
-            @pl.when(o != hub)
-            def _():
-                from_hub(yi, c, 0, c_peer).wait_recv()
-
-            @pl.when(ox == hub)
-            def _():
-                from_hub(yi, c, 1, c_peer).start()
+    strips = [(b, i) for b in range(2) for i in range(2)]
+
+    def load(n):
+        b, i = strips[n]
+        place = (b, pl.ds(i * strip, strip), slice(None))
+        return pltpu.make_async_copy(weight.at[place], held_weight.at[place], w_sem.at[n])
+
+    for n in range(4):
+        load(n).start()
+
+    def multiply(n):
+        b, i = strips[n]
+        load(n).wait()
+        total = jnp.zeros((raw.shape[1], strip), jnp.float32)
+        for k in range(2):
+            total += lax.dot_general(
+                raw[k],
+                held_weight[b, pl.ds(i * strip, strip), pl.ds(k * block, block)],
+                (((1,), (1,)), ((), ())),
+                preferred_element_type=jnp.float32,
+            )
+        product[b, :, pl.ds(i * strip, strip)] = total.astype(product.dtype)
+
+    def act_step(c, condition):
+        @pl.when(condition & here)
+        def _():
+            own_act(c).wait()
+
+        @pl.when(condition & jnp.logical_not(here))
+        def _():
+            over_x(c).wait_recv()
+
+        @pl.when(condition & is_hub)
+        def _():
+            over_x(c).start()
+
+        @pl.when(condition)
+        def _():
+            over_core(c).start()
 
     for c in range(CHUNKS):
         for b in range(2):
@@ -346,17 +366,20 @@
                 remote(ref, ref, g_send.at[0], g_recv.at[b * CHUNKS + c], c_peer).wait_recv()
                 y_copy(ref, b, c).start()
 
-        hub_step(c)
-    raw_x.wait_recv()
-    raw_xc.start()
+        act_step(c, is_hub)
+        if c == 1:
+            raw_x.wait_recv()
+            raw_xc.start()
+        if c == 2:
+            raw_c.wait_recv()
+            raw_xc.wait()
+            raw_local.wait()
+        if 2 <= c < 6:
+            multiply(c - 2)
     for c in range(CHUNKS):
-        relay_step(c)
-    raw_c.wait_recv()
-    raw_xc.wait()
-    raw_x.wait_send()
-    raw_c.wait_send()
-    raw_local.wait()
+        act_step(c, not_hub)
     for c in range(CHUNKS):
+        over_core(c).wait()
         for b in range(2):
             ref = g_tile(b, 1 - y, c)
             remote(ref, ref, y_send.at[0], y_recv.at[b * CHUNKS + c], c_peer).wait_recv()
@@ -368,22 +391,19 @@
                 to_plane(c, j).wait_send()
             own_grad(c).wait()
 
-        @pl.when(jnp.logical_not(is_grad) & jnp.logical_not(stays))
+        @pl.when(is_act & jnp.logical_not(stays))
         def _():
             to_hub(c).wait_send()
 
-        for yi in range(2):
-
-            @pl.when(o == hub)
-            def _():
-                from_hub(yi, c, 0, x_peer).wait_send()
-
-            @pl.when((o == hub) | (ox == hub))
-            def _():
-                from_hub(yi, c, 1, c_peer).wait_send()
-
-
-def deliver(low, pieces):
+        @pl.when(is_hub)
+        def _():
+            over_x(c).wait_send()
+
+    raw_x.wait_send()
+    raw_c.wait_send()
+
+
+def deliver(low, pieces, weight):
     tokens, part = low.shape
     _, rows, width = pieces.shape
     dma = pltpu.SemaphoreType.DMA
@@ -393,11 +413,14 @@
         out_shape=(
             jax.ShapeDtypeStruct((2, tokens, 2 * part), low.dtype),
             jax.ShapeDtypeStruct((tokens, 2 * part), low.dtype),
-            jax.ShapeDtypeStruct((2, rows, 4 * width), low.dtype),
+            jax.ShapeDtypeStruct((2, rows, width), low.dtype),
         ),
-        in_specs=[vmem, vmem],
+        in_specs=[vmem, vmem, pl.BlockSpec(memory_space=pl.ANY)],
         out_specs=(vmem, vmem, vmem),
         scratch_shapes=[
+            pltpu.VMEM((2, rows, 4 * width), low.dtype),
+            pltpu.VMEM(weight.shape, weight.dtype),
+            dma((4,)),
             dma((4,)),
             dma((3,)),
             dma((3 * CHUNKS,)),
@@ -405,14 +428,15 @@
             dma((2 * CHUNKS,)),
             dma((2 * CHUNKS,)),
             dma((CHUNKS,)),
-            dma((2 * CHUNKS,)),
-            dma((4 * CHUNKS,)),
-            dma((2 * CHUNKS,)),
+            dma((CHUNKS,)),
+            dma((CHUNKS,)),
+            dma((CHUNKS,)),
+            dma((CHUNKS,)),
             dma((CHUNKS,)),
         ],
         compiler_params=pltpu.CompilerParams(collective_id=1, has_side_effects=True),
         name="deliver",
-    )(low, pieces)
+    )(low, pieces, weight)
 
 
 def whiten_kernel(sides, out, gram, low, ray, head, tail, left, right):
@@ -462,7 +486,9 @@
     scale = moment(2 * POWER - 1) / moment(2 * POWER - 2)
     inverse = 1.0 / scale
     root = 1.0 / jnp.sqrt(scale)
-    start = lax.axis_index("out") * (2 * part) + lax.axis_index("grp") * part
+    z, o, y = lax.axis_index("tok"), lax.axis_index("out"), lax.axis_index("grp")
+    act_start = 2 * (o // 2 * 2 + y) + lax.rem(o, 2)
+    start = jnp.where((z == 1) | (z == 2), 2 * o + y, act_start) * part
     cols = pl.ds(pl.multiple_of(start, part), part)
 
     @pl.loop(0, steps)
@@ -519,18 +545,14 @@
 
 
 def planes(activations, out_grads, weight):
-    tok_dev, blocks, width = activations.shape
-    block = width * lax.axis_size("out")
+    tok_dev, _, width = activations.shape
     part = width // lax.axis_size("grp")
     token_count = tok_dev * lax.axis_size(("tok", "grp"))
     pieces = jnp.swapaxes(jnp.concatenate([activations, out_grads], axis=1), 0, 1)
-    grads_low, acts_low, grads_whole = deliver(whiten(collect(pieces), part), pieces)
+    grads_low, acts_low, product = deliver(whiten(collect(pieces), part), pieces, weight)
     update = jnp.einsum("ta,btc->abc", acts_low, grads_low, preferred_element_type=jnp.float32)
     update = (update / math.sqrt(token_count)).astype(jnp.bfloat16)
-    weight_rows = weight.reshape(blocks, width, blocks, block)
-    input_grad = jnp.einsum(
-        "jtq,bcjq->tbc", grads_whole, weight_rows, preferred_element_type=jnp.float32
-    ).astype(jnp.bfloat16)
+    input_grad = jnp.swapaxes(product, 0, 1)
     return (update, input_grad)
 
 

time: 102 us -> 94.5 us (0.926)
  matrix products: 9.52 us -> 3.19 us
    dot_general x1 -> x0, matrix products: 6.33 us -> none  [planes(): jnp.einsum('jtq,bcjq->tbc', grads_whole, weight_rows, preferred_element_t...]
where the time goes in v4:
time: 94.5 us; the launch traced here: 94.2 us
  Pallas kernels  84.5 us (89%)
  local copies, waits for them, and re-layouts  4.99 us (5%)
  matrix products  3.19 us (3%)
    pallas_call x1, Pallas kernels, deliver(): pl.pallas_call(deliver_kernel, out_shape=(jax.ShapeDtypeStruct((2, tokens...  38.1 us
    pallas_call x1, Pallas kernels, collect(): pl.pallas_call(collect_kernel, out_shape=jax.ShapeDtypeStruct((rows * 8,...  31.3 us
    pallas_call x1, Pallas kernels, whiten(): pl.pallas_call(whiten_kernel, out_shape=jax.ShapeDtypeStruct((tokens, par...  15.2 us
    unnamed x6, local copies, waits for them, and re-layouts  4.99 us
    dot_general x1, matrix products, planes(): jnp.einsum('ta,btc->abc', acts_low, grads_low, preferred_element_type=jnp...  3.19 us

profile of v4, /device:TPU:0, one launch (start us, length us, event | category | flops | bytes accessed | tf_op | source)
XLA Modules:
  0.0 94.2 jit_solution(12523003386518603095)
XLA Ops:
  0.6 1.0 %copy.5 = bf16[128,2,512]{2,0,1:T(8,128)(2,1)S(1)} copy(bf16[128,2,512]{2,1,0:T(2,128)(2,1)} %param.3) | data formatting | bytes 524288 | tf_op args[0]
  1.6 1.0 %copy.6 = bf16[128,2,512]{2,0,1:T(8,128)(2,1)S(1)} copy(bf16[128,2,512]{2,1,0:T(2,128)(2,1)} %param.4) | data formatting | bytes 524288 | tf_op args[1]
  2.6 0.8 maximum_bitcast_fusion.pieces
  3.4 31.3 %collect.1.sides = bf16[1024,2048]{1,0:T(8,128)(2,1)} custom-call(bf16[4,128,512]{2,1,0:T(8,128)(2,1)} %maximum_bitcast_fusion.pieces), custom_call_target="tpu_custom_call" | custom-call | tf_op jit(solution)/shard_map/collect/pallas_call | solution.py:215
  34.7 15.2 %whiten.1.low = bf16[1024,256]{1,0:T(8,128)(2,1)} custom-call(bf16[1024,2048]{1,0:T(8,128)(2,1)} %collect.1.sides), custom_call_target="tpu_custom_call" | custom-call | tf_op jit(solution)/shard_map/whiten/pallas_call | solution.py:529
  49.9 38.1 %deliver.1 = (bf16[2,1024,512]{2,1,0:T(8,128)(2,1)}, bf16[1024,512]{1,0:T(8,128)(2,1)}, bf16[2,128,512]{2,1,0:T(8,128)(2,1)}) custom-call(bf16[1024,256]{1,0:T(8,128)(2,1)} %whiten.1.low, bf16[4,128,512]{2,1,0:T(8,128)(2,1)} %maximum_bitcast_fusion.pieces, bf16[2,512,4096]{2,1,0:T(8,128)(2,1)} %weight.1), custom_call_target="tpu_custom_call" | custom-call | tf_op jit(solution)/shard_map/deliver/pallas_call | solution.py:411
  88.0 3.2 %multiply_convert_fusion = bf16[512,2,512]{2,0,1:T(8,128)(2,1)S(1)} fusion(bf16[2,1024,512]{2,1,0:T(8,128)(2,1)} %get-tuple-element.6, bf16[1024,512]{1,0:T(8,128)(2,1)} %get-tuple-element.5), kind=kOutput, calls=%fused_computation | convolution fusion | flops 1074790400 | bytes 4194304 | tf_op jit(solution)/shard_map/ta,btc->abc/dot_general | solution.py:553
  91.2 0.0 copy-start
  91.2 2.0 %copy.8 = bf16[512,2,512]{2,1,0:T(2,128)(2,1)} copy(bf16[512,2,512]{2,0,1:T(8,128)(2,1)S(1)} %multiply_convert_fusion) | data formatting | bytes 2097152
  93.2 0.0 copy-done
  93.2 1.0 %copy.9 = bf16[128,2,512]{2,1,0:T(2,128)(2,1)} copy(bf16[128,2,512]{2,0,1:T(8,128)(2,1)S(1)} %bitcast.7) | data formatting | bytes 524288
Async XLA Ops:
  91.2 2.1 %copy-start = (bf16[2,128,512]{2,1,0:T(8,128)(2,1)S(1)}, bf16[2,128,512]{2,1,0:T(8,128)(2,1)}, u32[]{:S(2)}) copy-start(bf16[2,128,512]{2,1,0:T(8,128)(2,1)} %get-tuple-element.7) | copy-start | bytes 786436

commit v5 on v4

--- a/solution.py
+++ b/solution.py
@@ -133,7 +133,7 @@
 
 
 def held(z):
-    return z + (z + 2) // 3 - 3 * (z // 3)
+    return z + 2 - 3 * ((z + 2) // 3) + z // 3
 
 
 def neighbours():
@@ -230,7 +230,7 @@
 def deliver_kernel(
     low, pieces, weight, grads, acts, product,
     raw, held_weight, w_sem, r_send, r_recv, g_send, y_send, g_recv, y_recv,
-    a_send, a_recv, x_send, c_send, c_recv, local,
+    a_send, a_recv, x_send, x_recv, c_send, c_recv, local,
 ):
     z, o, y, ox, oc, zs, z_peers, y_peer, x_peer, c_peer = neighbours()
     tokens, part = low.shape
@@ -238,15 +238,15 @@
     width = pieces.shape[2]
     block = raw.shape[2]
     strip = width // 2
-    is_grad = (z == 1) | (z == 2)
+    is_grad = (z == 0) | (z == 3)
     is_act = jnp.logical_not(is_grad)
-    mine = z - 1
-    h = lax.rem(o, 2)
-    goal_z = (z // 3) * 2 + o // 2
+    mine = z // 3
+    h = o // 2
+    goal_z = (z // 2) * 2 + lax.rem(o, 2)
     stays = goal_z == z
     goal = {"tok": goal_z, "out": o, "grp": y}
-    is_hub = o // 2 == lax.rem(z, 2)
-    not_hub = jnp.logical_not(is_hub)
+    onward = ({"tok": lax.rem(z + 1, 4), "out": o, "grp": y}, {"tok": lax.rem(z + 3, 4), "out": o, "grp": y})
+    is_hub = lax.rem(o, 2) == lax.rem(z, 2)
     here = is_act & stays
     greet(z_peers + [y_peer, x_peer, c_peer])
 
@@ -283,10 +283,8 @@
     def own_act(c):
         return pltpu.make_async_copy(piece(c), a_tile(h, c), local.at[c])
 
-    def to_plane(c, j):
-        return remote(
-            piece(c), g_tile(mine, y, c), g_send.at[c * 3 + j - 1], g_recv.at[mine * CHUNKS + c], z_peers[j - 1]
-        )
+    def to_plane(src, b, c):
+        return remote(src, g_tile(b, y, c), g_send.at[b * CHUNKS + c], g_recv.at[b * CHUNKS + c], onward[b])
 
     def y_copy(src, b, c):
         return remote(src, g_tile(b, y, c), y_send.at[b * CHUNKS + c], y_recv.at[b * CHUNKS + c], y_peer)
@@ -294,19 +292,23 @@
     def to_hub(c):
         return remote(piece(c), a_tile(h, c), a_send.at[c], a_recv.at[c], goal)
 
-    def over_x(c):
-        return remote(a_tile(h, c), a_tile(h, c), x_send.at[c], a_recv.at[c], x_peer)
-
-    def over_core(c):
-        return remote(a_tile(h, c), a_tile(h, c), c_send.at[c], c_recv.at[c], c_peer)
+    def over_x(c, i):
+        return remote(a_tile(i, c), a_tile(i, c), x_send.at[c], x_recv.at[c], x_peer)
+
+    def over_core(c, i):
+        place = i * CHUNKS + c
+        return remote(a_tile(i, c), a_tile(i, c), c_send.at[place], c_recv.at[place], c_peer)
 
     for c in range(CHUNKS):
+        for b in range(2):
+
+            @pl.when(z == 3 * b)
+            def _():
+                to_plane(piece(c), b, c).start()
+                y_copy(piece(c), b, c).start()
 
         @pl.when(is_grad)
         def _():
-            for j in (1, 3, 2):
-                to_plane(c, j).start()
-            y_copy(piece(c), mine, c).start()
             own_grad(c).start()
 
         @pl.when(here)
@@ -340,33 +342,44 @@
             )
         product[b, :, pl.ds(i * strip, strip)] = total.astype(product.dtype)
 
-    def act_step(c, condition):
-        @pl.when(condition & here)
+    def hub_step(c):
+        @pl.when(here)
         def _():
             own_act(c).wait()
 
-        @pl.when(condition & jnp.logical_not(here))
-        def _():
-            over_x(c).wait_recv()
-
-        @pl.when(condition & is_hub)
-        def _():
-            over_x(c).start()
-
-        @pl.when(condition)
-        def _():
-            over_core(c).start()
+        @pl.when(is_hub & jnp.logical_not(here))
+        def _():
+            ref = a_tile(h, c)
+            remote(ref, ref, a_send.at[0], a_recv.at[c], c_peer).wait_recv()
+
+        @pl.when(is_hub)
+        def _():
+            over_x(c, h).start()
+            over_core(c, h).start()
+
+    def cross_step(c):
+        @pl.when(is_hub)
+        def _():
+            over_x(c, 1 - h).wait_recv()
+            over_core(c, 1 - h).start()
 
     for c in range(CHUNKS):
         for b in range(2):
 
-            @pl.when(z != b + 1)
+            @pl.when(z != 3 * b)
             def _():
                 ref = g_tile(b, y, c)
                 remote(ref, ref, g_send.at[0], g_recv.at[b * CHUNKS + c], c_peer).wait_recv()
-                y_copy(ref, b, c).start()
-
-        act_step(c, is_hub)
+
+            @pl.when((z != 3 * b) & (z != 3 - 3 * b))
+            def _():
+                to_plane(g_tile(b, y, c), b, c).start()
+
+            @pl.when(z != 3 * b)
+            def _():
+                y_copy(g_tile(b, y, c), b, c).start()
+
+        hub_step(c)
         if c == 1:
             raw_x.wait_recv()
             raw_xc.start()
@@ -377,27 +390,38 @@
         if 2 <= c < 6:
             multiply(c - 2)
     for c in range(CHUNKS):
-        act_step(c, not_hub)
+        cross_step(c)
     for c in range(CHUNKS):
-        over_core(c).wait()
         for b in range(2):
             ref = g_tile(b, 1 - y, c)
             remote(ref, ref, y_send.at[0], y_recv.at[b * CHUNKS + c], c_peer).wait_recv()
             y_copy(g_tile(b, y, c), b, c).wait_send()
 
+            @pl.when(z != 3 - 3 * b)
+            def _():
+                to_plane(g_tile(b, y, c), b, c).wait_send()
+
         @pl.when(is_grad)
         def _():
-            for j in (1, 3, 2):
-                to_plane(c, j).wait_send()
             own_grad(c).wait()
 
         @pl.when(is_act & jnp.logical_not(stays))
         def _():
             to_hub(c).wait_send()
 
+        for i in range(2):
+
+            @pl.when(is_hub)
+            def _():
+                over_core(c, i).wait_send()
+
+            @pl.when(jnp.logical_not(is_hub))
+            def _():
+                over_core(c, i).wait_recv()
+
         @pl.when(is_hub)
         def _():
-            over_x(c).wait_send()
+            over_x(c, h).wait_send()
 
     raw_x.wait_send()
     raw_c.wait_send()
@@ -423,7 +447,7 @@
             dma((4,)),
             dma((4,)),
             dma((3,)),
-            dma((3 * CHUNKS,)),
+            dma((2 * CHUNKS,)),
             dma((2 * CHUNKS,)),
             dma((2 * CHUNKS,)),
             dma((2 * CHUNKS,)),
@@ -431,7 +455,8 @@
             dma((CHUNKS,)),
             dma((CHUNKS,)),
             dma((CHUNKS,)),
-            dma((CHUNKS,)),
+            dma((2 * CHUNKS,)),
+            dma((2 * CHUNKS,)),
             dma((CHUNKS,)),
         ],
         compiler_params=pltpu.CompilerParams(collective_id=1, has_side_effects=True),
@@ -442,7 +467,7 @@
 def whiten_kernel(sides, out, gram, low, ray, head, tail, left, right):
     tokens, block = sides.shape
     part = out.shape[1]
-    tile = min(256, tokens)
+    tile = min(512, tokens)
     steps = tokens // tile
     across = (((1,), (1,)), ((), ()))
     ones = jnp.ones((8, block), sides.dtype)
@@ -487,8 +512,8 @@
     inverse = 1.0 / scale
     root = 1.0 / jnp.sqrt(scale)
     z, o, y = lax.axis_index("tok"), lax.axis_index("out"), lax.axis_index("grp")
-    act_start = 2 * (o // 2 * 2 + y) + lax.rem(o, 2)
-    start = jnp.where((z == 1) | (z == 2), 2 * o + y, act_start) * part
+    act_start = 2 * (lax.rem(o, 2) * 2 + y) + o // 2
+    start = jnp.where((z == 0) | (z == 3), 2 * o + y, act_start) * part
     cols = pl.ds(pl.multiple_of(start, part), part)
 
     @pl.loop(0, steps)

time: 94.5 us -> 133 us (1.41)
  Pallas kernels: 84.5 us -> 123 us
    pallas_call x1, Pallas kernels: 38.1 us -> 78.6 us  [deliver(): pl.pallas_call(deliver_kernel, out_shape=(jax.ShapeDtypeStruct((2, tokens...]
    pallas_call x1, Pallas kernels: 15.2 us -> 13.5 us  [whiten(): pl.pallas_call(whiten_kernel, out_shape=jax.ShapeDtypeStruct((tokens, par...]
where the time goes in v5:
time: 133 us
  Pallas kernels  123 us (92%)
  local copies, waits for them, and re-layouts  4.99 us (4%)
  matrix products  3.19 us (2%)
    pallas_call x1, Pallas kernels, deliver(): pl.pallas_call(deliver_kernel, out_shape=(jax.ShapeDtypeStruct((2, tokens...  78.6 us
    pallas_call x1, Pallas kernels, collect(): pl.pallas_call(collect_kernel, out_shape=jax.ShapeDtypeStruct((rows * 8,...  31.3 us
    pallas_call x1, Pallas kernels, whiten(): pl.pallas_call(whiten_kernel, out_shape=jax.ShapeDtypeStruct((tokens, par...  13.5 us
    unnamed x6, local copies, waits for them, and re-layouts  4.99 us
    dot_general x1, matrix products, planes(): jnp.einsum('ta,btc->abc', acts_low, grads_low, preferred_element_type=jnp...  3.19 us

profile of v5, /device:TPU:0, one launch (start us, length us, event | category | flops | bytes accessed | tf_op | source)
XLA Modules:
  0.0 133.0 jit_solution(140204789660894804)
XLA Ops:
  0.6 1.0 copy.5
  1.6 1.0 copy.6
  2.6 0.8 maximum_bitcast_fusion.pieces
  3.4 31.3 %collect.1.sides = bf16[1024,2048]{1,0:T(8,128)(2,1)} custom-call(bf16[4,128,512]{2,1,0:T(8,128)(2,1)} %maximum_bitcast_fusion.pieces), custom_call_target="tpu_custom_call" | custom-call | tf_op jit(solution)/shard_map/collect/pallas_call | solution.py:215
  34.7 13.5 %whiten.1.low = bf16[1024,256]{1,0:T(8,128)(2,1)} custom-call(bf16[1024,2048]{1,0:T(8,128)(2,1)} %collect.1.sides), custom_call_target="tpu_custom_call" | custom-call | tf_op jit(solution)/shard_map/whiten/pallas_call | solution.py:554
  48.2 78.6 %deliver.1 = (bf16[2,1024,512]{2,1,0:T(8,128)(2,1)}, bf16[1024,512]{1,0:T(8,128)(2,1)}, bf16[2,128,512]{2,1,0:T(8,128)(2,1)}) custom-call(bf16[1024,256]{1,0:T(8,128)(2,1)} %whiten.1.low, bf16[4,128,512]{2,1,0:T(8,128)(2,1)} %maximum_bitcast_fusion.pieces, bf16[2,512,4096]{2,1,0:T(8,128)(2,1)} %weight.1), custom_call_target="tpu_custom_call" | custom-call | tf_op jit(solution)/shard_map/deliver/pallas_call | solution.py:435
  126.8 3.2 %multiply_convert_fusion = bf16[512,2,512]{2,0,1:T(8,128)(2,1)S(1)} fusion(bf16[2,1024,512]{2,1,0:T(8,128)(2,1)} %get-tuple-element.6, bf16[1024,512]{1,0:T(8,128)(2,1)} %get-tuple-element.5), kind=kOutput, calls=%fused_computation | convolution fusion | flops 1074790400 | bytes 4194304 | tf_op jit(solution)/shard_map/ta,btc->abc/dot_general | solution.py:578
  130.0 0.0 copy-start
  130.0 2.0 %copy.8 = bf16[512,2,512]{2,1,0:T(2,128)(2,1)} copy(bf16[512,2,512]{2,0,1:T(8,128)(2,1)S(1)} %multiply_convert_fusion) | data formatting | bytes 2097152
  132.1 0.0 copy-done
  132.1 1.0 copy.9
Async XLA Ops:
  130.0 2.1 %copy-start = (bf16[2,128,512]{2,1,0:T(8,128)(2,1)S(1)}, bf16[2,128,512]{2,1,0:T(8,128)(2,1)}, u32[]{:S(2)}) copy-start(bf16[2,128,512]{2,1,0:T(8,128)(2,1)} %get-tuple-element.7) | copy-start | bytes 786436

commit v6 on v5

--- a/solution.py
+++ b/solution.py
@@ -117,6 +117,7 @@
 HOPS = (0, 1, 3, 2)
 CHUNKS = 8
 SPLIT = 2
+LAG = 3
 
 
 def greet(peers):
@@ -245,7 +246,7 @@
     goal_z = (z // 2) * 2 + lax.rem(o, 2)
     stays = goal_z == z
     goal = {"tok": goal_z, "out": o, "grp": y}
-    onward = ({"tok": lax.rem(z + 1, 4), "out": o, "grp": y}, {"tok": lax.rem(z + 3, 4), "out": o, "grp": y})
+    near, far = z // 2, 1 - z // 2
     is_hub = lax.rem(o, 2) == lax.rem(z, 2)
     here = is_act & stays
     greet(z_peers + [y_peer, x_peer, c_peer])
@@ -284,7 +285,7 @@
         return pltpu.make_async_copy(piece(c), a_tile(h, c), local.at[c])
 
     def to_plane(src, b, c):
-        return remote(src, g_tile(b, y, c), g_send.at[b * CHUNKS + c], g_recv.at[b * CHUNKS + c], onward[b])
+        return remote(src, g_tile(b, y, c), g_send.at[b * CHUNKS + c], g_recv.at[b * CHUNKS + c], {"tok": lax.rem(z + 5 - 2 * b, 4), "out": o, "grp": y})
 
     def y_copy(src, b, c):
         return remote(src, g_tile(b, y, c), y_send.at[b * CHUNKS + c], y_recv.at[b * CHUNKS + c], y_peer)
@@ -363,32 +364,35 @@
             over_x(c, 1 - h).wait_recv()
             over_core(c, 1 - h).start()
 
-    for c in range(CHUNKS):
-        for b in range(2):
-
-            @pl.when(z != 3 * b)
+    def take(b, c):
+        ref = g_tile(b, y, c)
+        remote(ref, ref, g_send.at[0], g_recv.at[b * CHUNKS + c], c_peer).wait_recv()
+
+        @pl.when(is_act)
+        def _():
+            to_plane(ref, b, c).start()
+
+        y_copy(ref, b, c).start()
+
+    for step in range(CHUNKS + LAG):
+        if step < CHUNKS:
+
+            @pl.when(is_act)
             def _():
-                ref = g_tile(b, y, c)
-                remote(ref, ref, g_send.at[0], g_recv.at[b * CHUNKS + c], c_peer).wait_recv()
-
-            @pl.when((z != 3 * b) & (z != 3 - 3 * b))
-            def _():
-                to_plane(g_tile(b, y, c), b, c).start()
-
-            @pl.when(z != 3 * b)
-            def _():
-                y_copy(g_tile(b, y, c), b, c).start()
-
-        hub_step(c)
-        if c == 1:
+                take(near, step)
+
+            hub_step(step)
+        if step >= LAG:
+            take(far, step - LAG)
+        if step == 1:
             raw_x.wait_recv()
             raw_xc.start()
-        if c == 2:
+        if step == 2:
             raw_c.wait_recv()
             raw_xc.wait()
             raw_local.wait()
-        if 2 <= c < 6:
-            multiply(c - 2)
+        if 3 <= step < 7:
+            multiply(step - 3)
     for c in range(CHUNKS):
         cross_step(c)
     for c in range(CHUNKS):

time: 133 us -> 92.1 us (0.69); the launches traced: 133 us -> 90.3 us
  Pallas kernels: 123 us -> 80.6 us
    pallas_call x1, Pallas kernels: 78.6 us -> 35.9 us  [deliver(): pl.pallas_call(deliver_kernel, out_shape=(jax.ShapeDtypeStruct((2, tokens...]
where the time goes in v6:
time: 92.1 us; the launch traced here: 90.3 us
  Pallas kernels  80.6 us (88%)
  local copies, waits for them, and re-layouts  4.99 us (5%)
  matrix products  3.19 us (3%)
    pallas_call x1, Pallas kernels, deliver(): pl.pallas_call(deliver_kernel, out_shape=(jax.ShapeDtypeStruct((2, tokens...  35.9 us
    pallas_call x1, Pallas kernels, collect(): pl.pallas_call(collect_kernel, out_shape=jax.ShapeDtypeStruct((rows * 8,...  31.3 us
    pallas_call x1, Pallas kernels, whiten(): pl.pallas_call(whiten_kernel, out_shape=jax.ShapeDtypeStruct((tokens, par...  13.5 us
    unnamed x6, local copies, waits for them, and re-layouts  4.99 us
    dot_general x1, matrix products, planes(): jnp.einsum('ta,btc->abc', acts_low, grads_low, preferred_element_type=jnp...  3.19 us

profile of v6, /device:TPU:0, one launch (start us, length us, event | category | flops | bytes accessed | tf_op | source)
XLA Modules:
  0.0 90.3 jit_solution(602595944704955048)
XLA Ops:
  0.6 1.0 %copy.5 = bf16[128,2,512]{2,0,1:T(8,128)(2,1)S(1)} copy(bf16[128,2,512]{2,1,0:T(2,128)(2,1)} %param.3) | data formatting | bytes 524288 | tf_op args[0]
  1.6 1.0 %copy.6 = bf16[128,2,512]{2,0,1:T(8,128)(2,1)S(1)} copy(bf16[128,2,512]{2,1,0:T(2,128)(2,1)} %param.4) | data formatting | bytes 524288 | tf_op args[1]
  2.6 0.8 maximum_bitcast_fusion.pieces
  3.4 31.3 %collect.1.sides = bf16[1024,2048]{1,0:T(8,128)(2,1)} custom-call(bf16[4,128,512]{2,1,0:T(8,128)(2,1)} %maximum_bitcast_fusion.pieces), custom_call_target="tpu_custom_call" | custom-call | tf_op jit(solution)/shard_map/collect/pallas_call | solution.py:216
  34.7 13.5 %whiten.1.low = bf16[1024,256]{1,0:T(8,128)(2,1)} custom-call(bf16[1024,2048]{1,0:T(8,128)(2,1)} %collect.1.sides), custom_call_target="tpu_custom_call" | custom-call | tf_op jit(solution)/shard_map/whiten/pallas_call | solution.py:558
  48.2 35.9 %deliver.1 = (bf16[2,1024,512]{2,1,0:T(8,128)(2,1)}, bf16[1024,512]{1,0:T(8,128)(2,1)}, bf16[2,128,512]{2,1,0:T(8,128)(2,1)}) custom-call(bf16[1024,256]{1,0:T(8,128)(2,1)} %whiten.1.low, bf16[4,128,512]{2,1,0:T(8,128)(2,1)} %maximum_bitcast_fusion.pieces, bf16[2,512,4096]{2,1,0:T(8,128)(2,1)} %weight.1), custom_call_target="tpu_custom_call" | custom-call | tf_op jit(solution)/shard_map/deliver/pallas_call | solution.py:439
  84.1 3.2 %multiply_convert_fusion = bf16[512,2,512]{2,0,1:T(8,128)(2,1)S(1)} fusion(bf16[2,1024,512]{2,1,0:T(8,128)(2,1)} %get-tuple-element.6, bf16[1024,512]{1,0:T(8,128)(2,1)} %get-tuple-element.5), kind=kOutput, calls=%fused_computation | convolution fusion | flops 1074790400 | bytes 4194304 | tf_op jit(solution)/shard_map/ta,btc->abc/dot_general | solution.py:582
  87.3 0.0 copy-start
  87.3 2.0 %copy.8 = bf16[512,2,512]{2,1,0:T(2,128)(2,1)} copy(bf16[512,2,512]{2,0,1:T(8,128)(2,1)S(1)} %multiply_convert_fusion) | data formatting | bytes 2097152
  89.3 0.0 copy-done
  89.3 1.0 %copy.9 = bf16[128,2,512]{2,1,0:T(2,128)(2,1)} copy(bf16[128,2,512]{2,0,1:T(8,128)(2,1)S(1)} %bitcast.7) | data formatting | bytes 524288
Async XLA Ops:
  87.3 2.1 %copy-start = (bf16[2,128,512]{2,1,0:T(8,128)(2,1)S(1)}, bf16[2,128,512]{2,1,0:T(8,128)(2,1)}, u32[]{:S(2)}) copy-start(bf16[2,128,512]{2,1,0:T(8,128)(2,1)} %get-tuple-element.7) | copy-start | bytes 786436
